TPU v7x, 32 devices: a whole 2x2x4 slice. The times are simulated.
32 devices in a mesh: tg: 4 (over z), pp: 2 (over y), grp: 4 (over x, core).
Axes of the slice: x: 2, y: 2, z: 4, core: 2. Of those that a mesh axis runs over, the one named last changes fastest.
Arguments:
- hidden_in: bfloat16 [512, 1024], P(('pp', 'grp'))
- seq_lens: int32 [512], P(('pp', 'grp'))
- k_cache: bfloat16 [2, 512, 128, 16, 64], P(None, ('pp', 'grp'), None, 'tg')
- v_cache: bfloat16 [2, 512, 128, 16, 64], P(None, ('pp', 'grp'), None, 'tg')
- attn_gain: bfloat16 [2, 1024], P('pp')
- w_qkv: bfloat16 [2, 3072, 1024], P('pp', ('tg', 'grp'))
- w_o: bfloat16 [2, 1024, 1024], P('pp', None, ('tg', 'grp'))
- mlp_gain: bfloat16 [2, 1024], P('pp')
- w_gate_up: bfloat16 [2, 5632, 1024], P('pp', ('tg', 'grp'))
- w_down: bfloat16 [2, 1024, 2816], P('pp', None, ('tg', 'grp'))
Outputs:
- output 1: bfloat16 [512, 1024], P(('pp', 'grp'))
- output 2: bfloat16 [2, 512, 128, 16, 64], P(None, ('pp', 'grp'), None, 'tg')
- output 3: bfloat16 [2, 512, 128, 16, 64], P(None, ('pp', 'grp'), None, 'tg')
- output 4: bfloat16 [2, 3072, 1024], P(None, 'tg')
- output 5: bfloat16 [2, 5632, 1024], P(None, 'tg')
All inputs are finite; a program needn't handle non-finite values.
Results may differ from a plain program's by a relative error of at most 0.0151185.
Values are sent between devices in bfloat16 or wider.
A program may use at most 1 GiB of HBM per device.

v0:
```python
import jax
import jax.numpy as jnp
from jax import lax
from jax.sharding import NamedSharding, PartitionSpec as P

ROPE_THETA = 500000.0
NORM_EPS = 1e-5
MASK_FILL = -1e30
ROW_AXES = ("pp", "grp")
TRAIN_AXES = ("tg", "grp")


def rms_norm(hidden, gain_vec):
    hidden_f32 = hidden.astype(jnp.float32)
    inv_rms = lax.rsqrt(jnp.mean(hidden_f32 * hidden_f32, axis=-1, keepdims=True) + NORM_EPS)
    return (hidden_f32 * inv_rms * gain_vec.astype(jnp.float32)).astype(jnp.bfloat16)


def apply_rope(values, cos_t, sin_t):
    half_dim = values.shape[-1] // 2
    first_half = values[..., :half_dim]
    second_half = values[..., half_dim:]
    return jnp.concatenate([first_half * cos_t - second_half * sin_t, second_half * cos_t + first_half * sin_t], axis=-1)


def rope_tables(seq_lens, head_dim):
    inv_freq = jnp.power(ROPE_THETA, -jnp.arange(0, head_dim, 2).astype(jnp.float32) / head_dim)
    angles = seq_lens.astype(jnp.float32)[:, None] * inv_freq[None, :]
    return jnp.cos(angles), jnp.sin(angles)


def attend(query_vals, k_layer, v_layer, seq_lens):
    head_dim = query_vals.shape[-1]
    positions = jnp.arange(k_layer.shape[1])
    scores = jnp.einsum("bgrd,bsgd->bgrs", query_vals, k_layer, preferred_element_type=jnp.float32) * head_dim ** -0.5
    scores = jnp.where(positions <= seq_lens[:, None, None, None], scores, MASK_FILL)
    attn_probs = jax.nn.softmax(scores, axis=-1).astype(jnp.bfloat16)
    out_vals = jnp.einsum("bgrs,bsgd->bgrd", attn_probs, v_layer, preferred_element_type=jnp.float32)
    return out_vals.astype(jnp.bfloat16)


def regroup_weights(attn_gain, w_qkv, w_o, mlp_gain, w_gate_up, w_down, group_rep, head_dim):
    model_dim = w_qkv.shape[2]
    qkv_block = lax.all_gather(w_qkv[0], "grp", axis=0, tiled=True)
    blocks = qkv_block.reshape(-1, group_rep + 2, head_dim, model_dim)
    stage_qkv = jnp.concatenate([
        blocks[:, :group_rep].reshape(-1, model_dim),
        blocks[:, group_rep].reshape(-1, model_dim),
        blocks[:, group_rep + 1].reshape(-1, model_dim)], axis=0)
    gen_qkv = lax.all_gather(stage_qkv[None], "pp", axis=0, tiled=True)
    ffn_train = w_gate_up.shape[1] // 2
    gate_up = lax.all_gather(w_gate_up[0].reshape(2, ffn_train, model_dim), "grp", axis=1, tiled=True)
    gen_gate_up = lax.all_gather(gate_up.reshape(1, -1, model_dim), "pp", axis=0, tiled=True)
    gen_o = lax.all_gather(lax.all_gather(w_o, "grp", axis=2, tiled=True), "pp", axis=0, tiled=True)
    gen_down = lax.all_gather(lax.all_gather(w_down, "grp", axis=2, tiled=True), "pp", axis=0, tiled=True)
    gen_attn_gain = lax.all_gather(attn_gain, "pp", axis=0, tiled=True)
    gen_mlp_gain = lax.all_gather(mlp_gain, "pp", axis=0, tiled=True)
    return gen_qkv, gen_o, gen_gate_up, gen_down, gen_attn_gain, gen_mlp_gain


def solution(mesh):
    merge_size = mesh.shape["grp"]
    cache_spec = P(None, ROW_AXES, None, "tg", None)
    in_specs = (P(ROW_AXES, None), P(ROW_AXES), cache_spec, cache_spec,
                P("pp", None), P("pp", TRAIN_AXES, None), P("pp", None, TRAIN_AXES),
                P("pp", None), P("pp", TRAIN_AXES, None), P("pp", None, TRAIN_AXES))
    out_specs = (P(ROW_AXES, None), cache_spec, cache_spec, P(None, "tg", None), P(None, "tg", None))

    def body(hidden_in, seq_lens, k_cache, v_cache, attn_gain, w_qkv, w_o, mlp_gain, w_gate_up, w_down):
        batch_loc = hidden_in.shape[0]
        layers = k_cache.shape[0]
        kv_loc = k_cache.shape[3]
        head_dim = k_cache.shape[4]
        heads_loc = w_o.shape[2] * merge_size // head_dim
        group_rep = heads_loc // kv_loc
        gen_qkv, gen_o, gen_gate_up, gen_down, gen_attn_gain, gen_mlp_gain = regroup_weights(
            attn_gain, w_qkv, w_o, mlp_gain, w_gate_up, w_down, group_rep, head_dim)
        q_rows = heads_loc * head_dim
        kv_rows = kv_loc * head_dim
        ffn_loc = gen_gate_up.shape[1] // 2
        cos_t, sin_t = rope_tables(seq_lens, head_dim)
        row_ids = jnp.arange(batch_loc)
        hidden = hidden_in
        for layer_idx in range(layers):
            normed = rms_norm(hidden, gen_attn_gain[layer_idx])
            qkv_proj = jnp.einsum("bd,rd->br", normed, gen_qkv[layer_idx], preferred_element_type=jnp.float32)
            query_vals = apply_rope(qkv_proj[:, :q_rows].reshape(batch_loc, kv_loc, group_rep, head_dim),
                                    cos_t[:, None, None, :], sin_t[:, None, None, :]).astype(jnp.bfloat16)
            key_new = apply_rope(qkv_proj[:, q_rows:q_rows + kv_rows].reshape(batch_loc, kv_loc, head_dim),
                                 cos_t[:, None, :], sin_t[:, None, :]).astype(jnp.bfloat16)
            value_new = qkv_proj[:, q_rows + kv_rows:].reshape(batch_loc, kv_loc, head_dim).astype(jnp.bfloat16)
            k_cache = k_cache.at[layer_idx, row_ids, seq_lens].set(key_new)
            v_cache = v_cache.at[layer_idx, row_ids, seq_lens].set(value_new)
            attn_out = attend(query_vals, k_cache[layer_idx], v_cache[layer_idx], seq_lens).reshape(batch_loc, q_rows)
            tp_part = jnp.einsum("bk,dk->bd", attn_out, gen_o[layer_idx], preferred_element_type=jnp.float32)
            hidden = (hidden.astype(jnp.float32) + lax.psum(tp_part, "tg")).astype(jnp.bfloat16)
            normed = rms_norm(hidden, gen_mlp_gain[layer_idx])
            gate_up = jnp.einsum("bd,rd->br", normed, gen_gate_up[layer_idx], preferred_element_type=jnp.float32)
            act_vals = (jax.nn.silu(gate_up[:, :ffn_loc]) * gate_up[:, ffn_loc:]).astype(jnp.bfloat16)
            tp_part = jnp.einsum("bf,df->bd", act_vals, gen_down[layer_idx], preferred_element_type=jnp.float32)
            hidden = (hidden.astype(jnp.float32) + lax.psum(tp_part, "tg")).astype(jnp.bfloat16)
        return hidden, k_cache, v_cache, gen_qkv, gen_gate_up

    return jax.shard_map(body, mesh=mesh, in_specs=in_specs, out_specs=out_specs, check_vma=False)
```

profile of v0, /device:TPU:0, one launch (start us, length us, event | category | flops | bytes accessed | tf_op | source)
XLA Modules:
  0.0 494.9 jit_solution(3039804860717001286)
XLA Ops:
  7.2 0.7 all-gather.22.cloned.1.call-update
  8.0 23.8 %all-gather.22.cloned.1.call-done = bf16[1,768,1024]{2,1,0:T(8,128)(2,1)} async-done(((bf16[1,192,1024]{2,1,0:T(8,128)(2,1)}), bf16[1,768,1024]{2,1,0:T(8,128)(2,1)}) %all-gather.22.cloned.1.call-update) | async-done | bytes 1572880 | tf_op jit(solution)/shard_map/all_gather | solution.py:44
  31.8 1.5 fusion.111
  33.2 1.3 pad_maximum_fusion
  34.6 7.2 %all_gather.33 = bf16[1,1024,256]{1,2,0:T(8,128)(2,1)S(1)} all-gather(bf16[1,1024,64]{1,2,0:T(8,128)(2,1)} %param.16), channel_id=1, replica_groups=mesh['tg'=4,'pp'=2,'grp'=4] {'grp'}, dimensions={2}, use_global_device_ids=true | all-gather | bytes 655360 | tf_op jit(solution)/shard_map/all_gather | solution.py:54
  41.7 1.0 copy.39
  42.8 0.5 all-gather.14.cloned.1.call-update
  43.4 0.5 all-gather.18.cloned.1.call-update
  44.1 4.6 all-gather.2
  48.7 0.1 fusion.32
  48.8 24.0 %copy.37 = bf16[2,64,128,4,64]{4,3,2,1,0:T(4,128)(2,1)} copy(bf16[2,64,128,4,64]{2,4,3,1,0:T(8,128)(2,1)} %param.12) | data formatting | bytes 16777216 | tf_op args[2]
  72.9 24.0 %copy.38 = bf16[2,64,128,4,64]{4,3,2,1,0:T(4,128)(2,1)} copy(bf16[2,64,128,4,64]{2,4,3,1,0:T(8,128)(2,1)} %param.13) | data formatting | bytes 16777216 | tf_op args[3]
  96.9 0.2 multiply_cosine_fusion
  97.1 2.0 fusion.16
  99.3 0.2 subtract_convert_fusion.2
  99.5 0.1 pad_maximum_fusion.1
  99.6 8.0 %scatter_fusion = bf16[2,64,128,4,64]{4,3,2,1,0:T(4,128)(2,1)} fusion(bf16[2,64,128,4,64]{4,3,2,1,0:T(4,128)(2,1)} %copy.37, s32[64]{0:T(128)S(1)} %get-tuple-element.53, bf16[64,4,64]{2,1,0:T(4,128)(2,1)S(1)} %pad_maximum_fusion.1), kind=kCustom, calls=%fused_computation | custom fusion | bytes 99072 | tf_op jit(solution)/shard_map/scatter | solution.py:92
  107.6 8.1 %slice_bitcast_fusion.3 = bf16[64,128,4,64]{3,2,1,0:T(4,128)(2,1)} fusion(bf16[2,64,128,4,64]{4,3,2,1,0:T(4,128)(2,1)} %scatter_fusion), kind=kLoop, calls=%fused_computation.11 | loop fusion | bytes 8388608 | tf_op jit(solution)/shard_map/squeeze | solution.py:94
  115.7 0.2 fusion.80
  115.9 0.1 maximum_bitcast_fusion
  116.0 7.8 %fusion.10 = f32[64,4,1,128]{3,2,1,0:T(1,128)S(1)} fusion(bf16[64,128,4,64]{3,2,1,0:T(4,128)(2,1)} %slice_bitcast_fusion.3, bf16[64,4,64,1]{2,1,0,3:T(4,128)(2,1)S(1)} %maximum_bitcast_fusion), kind=kOutput, calls=%fused_computation.18 | convolution fusion | flops 4194304 | bytes 4358144 | tf_op jit(solution)/shard_map/bgrd,bsgd->bgrs/dot_general | solution.py:35
  123.8 0.1 reshape.289
  123.9 8.1 %scatter_fusion.1 = bf16[2,64,128,4,64]{4,3,2,1,0:T(4,128)(2,1)} fusion(bf16[2,64,128,4,64]{4,3,2,1,0:T(4,128)(2,1)} %copy.38, s32[64]{0:T(128)S(1)} %get-tuple-element.53, bf16[64,4,64]{2,1,0:T(4,128)(2,1)S(1)} %reshape.289), kind=kCustom, calls=%fused_computation.1 | custom fusion | bytes 99072 | tf_op jit(solution)/shard_map/scatter | solution.py:93
  132.0 0.2 fusion.28
  132.2 5.4 %slice_bitcast_fusion.2 = bf16[64,128,4,64]{3,2,1,0:T(4,128)(2,1)S(1)} fusion(bf16[2,64,128,4,64]{4,3,2,1,0:T(4,128)(2,1)} %scatter_fusion.1), kind=kLoop, calls=%fused_computation.10 | loop fusion | bytes 8388608 | tf_op jit(solution)/shard_map/squeeze | solution.py:94
  137.6 2.3 fusion.8
  140.0 2.2 fusion.31
  142.3 0.7 all-gather.16.cloned.1.call-update
  143.1 8.3 %all-gather.18.cloned.1.call-done = bf16[1,1024,704]{1,2,0:T(8,128)(2,1)} async-done(((bf16[1,1024,176]{1,2,0:T(8,128)(2,1)}), bf16[1,1024,704]{1,2,0:T(8,128)(2,1)}) %all-gather.18.cloned.1.call-update) | async-done | bytes 1441808 | tf_op jit(solution)/shard_map/all_gather | solution.py:55
  151.4 4.3 all-gather.3
  155.8 33.8 %all-reduce.5.cloned.1.call-done = f32[64,1024]{1,0:T(8,128)} async-done(((f32[64,1024]{1,0:T(8,128)}), f32[64,1024]{1,0:T(8,128)}) %all-reduce.5.cloned.1.call-update) | async-done | bytes 262160 | tf_op jit(solution)/shard_map/psum | solution.py:96
  189.6 1.1 fusion.36
  190.7 75.2 %all-gather.16.cloned.1.call-done = bf16[2,1408,1024]{2,1,0:T(8,128)(2,1)} async-done(((bf16[1,1408,1024]{2,1,0:T(8,128)(2,1)}), bf16[2,1408,1024]{2,1,0:T(8,128)(2,1)}) %all-gather.16.cloned.1.call-update) | async-done | bytes 5767184 | tf_op jit(solution)/shard_map/all_gather | solution.py:53
  265.9 3.6 fusion.13
  269.5 40.0 %all-gather.20.cloned.1.call-done = bf16[2,1024,704]{1,2,0:T(8,128)(2,1)} async-done(((bf16[1,1024,704]{1,2,0:T(8,128)(2,1)}), bf16[2,1024,704]{1,2,0:T(8,128)(2,1)}) %all-gather.20.cloned.1.call-update) | async-done | bytes 2883600 | tf_op jit(solution)/shard_map/all_gather | solution.py:55
  309.4 2.7 fusion.19
  312.1 0.2 all-reduce.9.cloned.1.call-start
  312.4 35.4 %all-reduce.7.cloned.1.call-done = f32[64,1024]{1,0:T(8,128)} async-done(((f32[64,1024]{1,0:T(8,128)}), f32[64,1024]{1,0:T(8,128)}) %all-reduce.7.cloned.1.call-update) | async-done | bytes 262160 | tf_op jit(solution)/shard_map/psum | solution.py:101
  347.8 1.1 fusion.40
  348.9 0.6 fusion.14
  349.5 0.6 fusion.112
  350.2 0.6 slice.275
  350.9 0.8 fusion.82
  351.7 0.9 reshape.275
  352.6 0.2 subtract_convert_fusion
  352.8 0.1 pad_maximum_fusion.2
  352.9 8.0 %scatter_fusion.2 = bf16[2,64,128,4,64]{4,3,2,1,0:T(4,128)(2,1)} fusion(bf16[2,64,128,4,64]{4,3,2,1,0:T(4,128)(2,1)} %scatter_fusion, s32[64]{0:T(128)S(1)} %get-tuple-element.52, bf16[64,4,64]{2,1,0:T(4,128)(2,1)S(1)} %pad_maximum_fusion.2), kind=kCustom, calls=%fused_computation.2 | custom fusion | bytes 99072 | tf_op jit(solution)/shard_map/scatter | solution.py:92
  361.0 5.4 %slice_bitcast_fusion.1 = bf16[64,128,4,64]{3,2,1,0:T(4,128)(2,1)S(1)} fusion(bf16[2,64,128,4,64]{4,3,2,1,0:T(4,128)(2,1)} %scatter_fusion.2), kind=kLoop, calls=%fused_computation.9 | loop fusion | bytes 8388608 | tf_op jit(solution)/shard_map/squeeze | solution.py:94
  366.4 0.1 maximum_bitcast_fusion.1
  366.5 5.1 %fusion.6 = f32[64,4,1,128]{3,2,1,0:T(1,128)} fusion(bf16[64,128,4,64]{3,2,1,0:T(4,128)(2,1)S(1)} %slice_bitcast_fusion.1, bf16[64,4,64,1]{2,1,0,3:T(4,128)(2,1)S(1)} %maximum_bitcast_fusion.1), kind=kOutput, calls=%fused_computation.14 | convolution fusion | flops 4194304 | bytes 4358144 | tf_op jit(solution)/shard_map/bgrd,bsgd->bgrs/dot_general | solution.py:35
  371.6 1.1 fusion.29
  372.8 8.0 %scatter_fusion.3 = bf16[2,64,128,4,64]{4,3,2,1,0:T(4,128)(2,1)} fusion(bf16[2,64,128,4,64]{4,3,2,1,0:T(4,128)(2,1)} %scatter_fusion.1, s32[64]{0:T(128)S(1)} %get-tuple-element.52, bf16[64,4,64]{2,1,0:T(4,128)(2,1)S(1)} %reshape.301), kind=kCustom, calls=%fused_computation.3 | custom fusion | bytes 99072 | tf_op jit(solution)/shard_map/scatter | solution.py:93
  380.9 5.4 %slice_bitcast_fusion = bf16[64,128,4,64]{3,2,1,0:T(4,128)(2,1)S(1)} fusion(bf16[2,64,128,4,64]{4,3,2,1,0:T(4,128)(2,1)} %scatter_fusion.3), kind=kLoop, calls=%fused_computation.8 | loop fusion | bytes 8388608 | tf_op jit(solution)/shard_map/squeeze | solution.py:94
  386.2 2.3 fusion.4
  388.7 2.0 fusion.30
  390.8 35.3 %all-reduce.9.cloned.1.call-done = f32[64,1024]{1,0:T(8,128)} async-done(((f32[64,1024]{1,0:T(8,128)}), f32[64,1024]{1,0:T(8,128)}) %all-reduce.9.cloned.1.call-update) | async-done | bytes 262160 | tf_op jit(solution)/shard_map/psum | solution.py:96
  426.1 1.1 fusion.44
  427.2 2.8 fusion.12
  430.0 2.5 fusion.18
  432.5 23.4 %copy.40 = bf16[2,64,128,4,64]{2,4,3,1,0:T(8,128)(2,1)} copy(bf16[2,64,128,4,64]{4,3,2,1,0:T(4,128)(2,1)} %scatter_fusion.2) | data formatting | bytes 16777216
  455.9 23.4 %copy.41 = bf16[2,64,128,4,64]{2,4,3,1,0:T(8,128)(2,1)} copy(bf16[2,64,128,4,64]{4,3,2,1,0:T(4,128)(2,1)} %scatter_fusion.3) | data formatting | bytes 16777216
  479.2 1.6 fusion.47
  480.9 1.7 copy.92
  482.5 5.8 %copy.93 = bf16[2,1408,1024]{2,1,0:T(8,128)(2,1)} copy(bf16[2,1408,1024]{2,1,0:T(8,128)(2,1)} %all-gather.16.cloned.1.call-done) | data formatting | bytes 11534336
  (55 shorter events, 1.5 us)
Async XLA Ops:
  7.2 36.8 %copy-start.6 = (s32[64]{0:T(128)S(1)}, s32[64]{0:T(128)}, u32[]{:S(2)}) copy-start(s32[64]{0:T(128)} %param.11) | copy-start | bytes 772
  7.2 36.9 %copy-start.4 = (bf16[1,1024]{1,0:T(2,128)(2,1)S(1)}, bf16[1,1024]{1,0:T(2,128)(2,1)}, u32[]{:S(2)}) copy-start(bf16[1,1024]{1,0:T(2,128)(2,1)} %param.14) | copy-start | bytes 6148
  7.2 41.5 %copy-start.1 = (bf16[64,1024]{1,0:T(8,128)(2,1)S(1)}, bf16[64,1024]{1,0:T(8,128)(2,1)}, u32[]{:S(2)}) copy-start(bf16[64,1024]{1,0:T(8,128)(2,1)} %param.10) | copy-start | bytes 393220
  7.2 24.6 %all-gather.22.cloned.1.call-start = ((), (), s32[]{:S(2)}) async-start(), calls=%async_computation.9 | async-start | bytes 1966080 | tf_op jit(solution)/shard_map/all_gather | solution.py:44
  7.9 89.2 %all-gather.24.cloned.1.call-start = ((), (), s32[]{:S(2)}) async-start(), calls=%async_computation.10 | async-start | bytes 4718592 | tf_op jit(solution)/shard_map/all_gather | solution.py:50
  34.5 105.5 %all-gather.12.cloned.1.call-start = ((), (), s32[]{:S(2)}) async-start(), calls=%async_computation | async-start | bytes 1572864 | tf_op jit(solution)/shard_map/all_gather | solution.py:54
  42.8 99.6 %all-gather.14.cloned.1.call-start = ((), (), s32[]{:S(2)}) async-start(), calls=%async_computation.2 | async-start | bytes 3604480 | tf_op jit(solution)/shard_map/all_gather | solution.py:52
  43.3 108.0 %all-gather.18.cloned.1.call-start = ((), (), s32[]{:S(2)}) async-start(), calls=%async_computation.4 | async-start | bytes 1802240 | tf_op jit(solution)/shard_map/all_gather | solution.py:55
  43.9 145.6 %all-reduce.5.cloned.1.call-start = ((), (), s32[]{:S(2)}) async-start(), calls=%async_computation.1 | async-start | bytes 524288 | tf_op jit(solution)/shard_map/psum | solution.py:96
  137.6 13.8 %copy-start.5 = (bf16[1,1024]{1,0:T(2,128)(2,1)S(1)}, bf16[1,1024]{1,0:T(2,128)(2,1)}, u32[]{:S(2)}) copy-start(bf16[1,1024]{1,0:T(2,128)(2,1)} %param.17) | copy-start | bytes 6148
  139.9 209.0 %copy-start = (bf16[1536,1024]{1,0:T(8,128)(2,1)S(1)}, bf16[1536,1024]{1,0:T(8,128)(2,1)}, u32[]{:S(2)}) copy-start(bf16[1536,1024]{1,0:T(8,128)(2,1)} %all-gather.24.cloned.1.call-done) | copy-start | bytes 9437188
  142.3 123.6 %all-gather.16.cloned.1.call-start = ((), (), s32[]{:S(2)}) async-start(), calls=%async_computation.3 | async-start | bytes 8650752 | tf_op jit(solution)/shard_map/all_gather | solution.py:53
  143.0 166.4 %all-gather.20.cloned.1.call-start = ((), (), s32[]{:S(2)}) async-start(), calls=%async_computation.5 | async-start | bytes 4325376 | tf_op jit(solution)/shard_map/all_gather | solution.py:55
  151.4 196.4 %all-reduce.7.cloned.1.call-start = ((), (), s32[]{:S(2)}) async-start(), calls=%async_computation.6 | async-start | bytes 524288 | tf_op jit(solution)/shard_map/psum | solution.py:101
  312.1 113.9 %all-reduce.9.cloned.1.call-start = ((), (), s32[]{:S(2)}) async-start(), calls=%async_computation.7 | async-start | bytes 524288 | tf_op jit(solution)/shard_map/psum | solution.py:96
  361.0 5.4 %copy-start.2 = (bf16[64,4,32]{2,1,0:T(4,128)(2,1)S(1)}, bf16[64,4,32]{2,1,0:T(4,128)(2,1)}, u32[]{:S(2)}) copy-start(bf16[64,4,32]{2,1,0:T(4,128)(2,1)} %get-tuple-element.35) | copy-start | bytes 49156
  366.4 6.3 %copy-start.3 = (bf16[64,256]{1,0:T(8,128)(2,1)S(1)}, bf16[64,256]{1,0:T(8,128)(2,1)}, u32[]{:S(2)}) copy-start(bf16[64,256]{1,0:T(8,128)(2,1)} %slice.275) | copy-start | bytes 98308
  390.7 88.5 %all-reduce.11.cloned.1.call-start = ((), (), s32[]{:S(2)}) async-start(), calls=%async_computation.8 | async-start | bytes 524288 | tf_op jit(solution)/shard_map/psum | solution.py:101
Sparse Core Ops, SparseCore 0:
  9.6 22.1 all-gather.21
  34.7 45.1 all-gather.23
  82.0 21.0 all-gather.11
  104.5 26.7 all-gather.13
  132.6 18.6 all-gather.17
  154.1 35.4 all-reduce.4
  191.1 74.7 all-gather.15
  267.4 41.9 all-gather.19
  312.3 35.4 all-reduce.6
  390.8 35.1 all-reduce.8
  432.6 35.1 all-reduce.10
where the time goes:
time: 498 us; the launch traced here: 495 us
  waiting for transfers between devices  254 us (51%)
  local copies, waits for them, and re-layouts  164 us (33%)
  matrix products  35.8 us (7%)
  blocking collectives  16.1 us (3%)
  between operations  14.2 us (3%)
  other arithmetic  9.78 us (2%)
    psum x4, waiting for transfers between devices, body(): lax.psum(tp_part, 'tg')  105 us
    unnamed x20, local copies, waits for them, and re-layouts  102 us
    all_gather x1, waiting for transfers between devices, regroup_weights(): lax.all_gather(gate_up.reshape(1, -1, model_dim), 'pp', axis=0, tiled=True)  75.2 us
    all_gather x1, waiting for transfers between devices, regroup_weights(): lax.all_gather(lax.all_gather(w_down, 'grp', axis=2, tiled=True), 'pp', a...  40 us
    all_gather x1, waiting for transfers between devices, regroup_weights(): qkv_block = lax.all_gather(w_qkv[0], 'grp', axis=0, tiled=True)  23.8 us
    scatter x2, local copies, waits for them, and re-layouts, body(): v_cache = v_cache.at[layer_idx, row_ids, seq_lens].set(value_new)  16.1 us
    scatter x2, local copies, waits for them, and re-layouts, body(): k_cache = k_cache.at[layer_idx, row_ids, seq_lens].set(key_new)  16 us
    squeeze x2, local copies, waits for them, and re-layouts, body(): k_cache[layer_idx]  13.4 us
  transfers between devices with their start and end apart: 11, of which 7 were waited for; matrix products, arithmetic and copies ran while one was open for 29% of the time, Pallas kernels for 0%

commit v1 on v0

v1 whole, which is shorter than its diff:
```python
import functools

import jax
import jax.numpy as jnp
from jax import lax
from jax.experimental import pallas as pl
from jax.experimental.pallas import tpu as pltpu
from jax.sharding import PartitionSpec as P

ROPE_THETA = 500000.0
NORM_EPS = 1e-5
MASK_FILL = -1e30
ROW_AXES = ("pp", "grp")
TRAIN_AXES = ("tg", "grp")
BF16 = jnp.bfloat16
F32 = jnp.float32
MESH = pl.DeviceIdType.MESH
ANY = pl.BlockSpec(memory_space=pl.ANY)
VMEM = pl.BlockSpec(memory_space=pltpu.VMEM)
SEQ_TILE = 16
HEAD_ROWS = 8


def norm_rows(hidden_f32, gain_row):
    inv_rms = lax.rsqrt(jnp.mean(hidden_f32 * hidden_f32, axis=-1, keepdims=True) + NORM_EPS)
    return (hidden_f32 * inv_rms * gain_row).astype(BF16)


def rows(ref, start, count):
    return ref.at[pl.ds(pl.multiple_of(start, 16), count), :]


class Place:
    def __init__(self, tg_size):
        self.tg_size = tg_size
        self.tg = lax.axis_index("tg")
        self.pp = lax.axis_index("pp")
        self.grp = lax.axis_index("grp")
        self.partner = self.grp + 1 - 2 * lax.rem(self.grp, 2)
        self.across = lax.rem(self.grp + 2, 4)
        self.diagonal = lax.rem(self.partner + 2, 4)
        self.stage = 1 - self.pp

    def tg_at(self, step):
        return lax.rem(self.tg + step, self.tg_size)

    def barrier(self, with_tg):
        sem = pltpu.get_barrier_semaphore()
        targets = [{"grp": self.partner}, {"grp": self.across}, {"pp": self.stage}]
        if with_tg:
            targets += [{"tg": self.tg_at(step)} for step in range(1, self.tg_size)]
        for target in targets:
            pl.semaphore_signal(sem, inc=1, device_id=target, device_id_type=MESH)
        pl.semaphore_wait(sem, len(targets))


def gather_sems(count):
    dma = pltpu.SemaphoreType.DMA
    return [dma((count,)), dma((count, 2)), dma((count, 2)), dma((count, 2, 2))]


class Gather:
    def __init__(self, place, sems, index, layer, own, buf, base, stride, count):
        self.place, self.layer, self.own, self.buf = place, layer, own, buf
        self.base, self.stride, self.count = base, stride, count
        local, ysem, xsem, psem = sems
        self.local = local.at[index]
        self.ysem = (ysem.at[index, 0], ysem.at[index, 1])
        self.xsem = (xsem.at[index, 0], xsem.at[index, 1])
        self.psem = [(psem.at[index, k, 0], psem.at[index, k, 1]) for k in range(2)]

    def at(self, grp):
        return rows(self.buf, self.base + grp * self.stride, self.count)

    def remote(self, src, grp, sems, target):
        return pltpu.make_async_remote_copy(
            src_ref=src, dst_ref=self.at(grp), send_sem=sems[0], recv_sem=sems[1],
            device_id=target, device_id_type=MESH)

    def local_copy(self):
        return pltpu.make_async_copy(self.own, self.at(self.place.grp), self.local)

    def y_copy(self):
        return self.remote(self.own, self.place.grp, self.ysem, {"pp": self.place.stage})

    def x_copy(self, grp):
        return self.remote(self.at(grp), grp, self.xsem, {"grp": self.place.across})

    def p_copy(self, grp, which):
        return self.remote(self.at(grp), grp, self.psem[which], {"grp": self.place.partner})

    def start(self):
        @pl.when(self.place.pp == self.layer)
        def _():
            self.y_copy().start()
            self.local_copy().start()

    def send(self):
        @pl.when(self.place.pp == self.layer)
        def _():
            self.local_copy().wait()

        @pl.when(self.place.pp != self.layer)
        def _():
            self.y_copy().wait_recv()

        self.x_copy(self.place.grp).start()
        self.p_copy(self.place.grp, 0).start()

    def forward(self):
        self.x_copy(self.place.across).wait_recv()
        self.p_copy(self.place.across, 1).start()

    def arrive(self):
        self.p_copy(self.place.partner, 0).wait_recv()
        self.p_copy(self.place.diagonal, 1).wait_recv()

    def finish(self):
        @pl.when(self.place.pp == self.layer)
        def _():
            self.y_copy().wait_send()

        self.x_copy(self.place.grp).wait_send()
        self.p_copy(self.place.grp, 0).wait_send()
        self.p_copy(self.place.across, 1).wait_send()


def each(units, what):
    for unit in units:
        getattr(unit, what)()


def row_blocks(kind, sizes):
    head_rows, ffn_rows, merge = sizes
    top = (ffn_rows // 2 + 15) // 16 * 16
    halves = [(0, top), (top, ffn_rows - top)]
    if kind == "qkv":
        return [(k * head_rows, k * merge * head_rows, head_rows, head_rows) for k in range(3)]
    if kind == "o":
        return [(0, 0, head_rows, head_rows)]
    if kind == "gate":
        return [(off, off, ffn_rows, count) for off, count in halves]
    if kind == "up":
        return [(ffn_rows + off, off, ffn_rows, count) for off, count in halves]
    return [(off, off, ffn_rows, count) for off, count in halves]


class SumOverTg:
    def __init__(self, place, part, slots, full, sems):
        self.place, self.part, self.slots, self.full = place, part, slots, full
        self.count = slots.shape[1]
        self.send, self.recv = sems

    def scatter_copy(self, step):
        peer = self.place.tg_at(step)
        return pltpu.make_async_remote_copy(
            src_ref=rows(self.part, peer * self.count, self.count), dst_ref=self.slots.at[step - 1],
            send_sem=self.send.at[0, step - 1], recv_sem=self.recv.at[0, step - 1],
            device_id={"tg": peer}, device_id_type=MESH)

    def spread_copy(self, step):
        own = rows(self.full, self.place.tg * self.count, self.count)
        return pltpu.make_async_remote_copy(
            src_ref=own, dst_ref=own,
            send_sem=self.send.at[1, step - 1], recv_sem=self.recv.at[1, step - 1],
            device_id={"tg": self.place.tg_at(step)}, device_id_type=MESH)

    def spread_wait(self, step):
        peer = self.place.tg_at(self.place.tg_size - step)
        block = rows(self.full, peer * self.count, self.count)
        pltpu.make_async_remote_copy(
            src_ref=block, dst_ref=block,
            send_sem=self.send.at[1, step - 1], recv_sem=self.recv.at[1, step - 1],
            device_id={"tg": peer}, device_id_type=MESH).wait_recv()

    def steps(self):
        return range(1, self.place.tg_size)

    def scatter_start(self):
        for step in self.steps():
            self.scatter_copy(step).start()

    def total(self):
        for step in self.steps():
            self.scatter_copy(step).wait_recv()
        out = self.part[pl.ds(pl.multiple_of(self.place.tg * self.count, self.count), self.count), :]
        for step in self.steps():
            out = out + self.slots[step - 1]
        return out

    def spread_start(self, block):
        self.full[pl.ds(pl.multiple_of(self.place.tg * self.count, self.count), self.count), :] = block
        for step in self.steps():
            self.scatter_copy(step).wait_send()
        for step in self.steps():
            self.spread_copy(step).start()

    def spread_finish(self):
        for step in self.steps():
            self.spread_wait(step)
        for step in self.steps():
            self.spread_copy(step).wait_send()


def dot_nt(lhs, rhs):
    return lax.dot_general(lhs, rhs, (((1,), (1,)), ((), ())), preferred_element_type=F32)


def dot_nn(lhs, rhs):
    return jnp.dot(lhs, rhs, preferred_element_type=F32)


def first_kernel(tg_size, sizes, hidden, attn_gain, mlp_gain, w_qkv, normed, gains, qkv_out,
                 qkv_buf, other_attn, other_mlp, gain_send, gain_recv, out_sem, *sems):
    place = Place(tg_size)
    units = [Gather(place, sems, k, 0, w_qkv.at[pl.ds(src, count), :], qkv_buf, base, stride, count)
             for k, (src, base, stride, count) in enumerate(row_blocks("qkv", sizes))]
    place.barrier(False)
    gain_copies = [
        pltpu.make_async_remote_copy(
            src_ref=src, dst_ref=dst, send_sem=gain_send.at[k], recv_sem=gain_recv.at[k],
            device_id={"pp": place.stage}, device_id_type=MESH)
        for k, (src, dst) in enumerate([(attn_gain, other_attn), (mlp_gain, other_mlp)])]
    for copy in gain_copies:
        copy.start()
    each(units, "start")
    for copy in gain_copies:
        copy.wait()
    first = place.pp == 0
    table = []
    for mine, other in [(attn_gain, other_attn), (mlp_gain, other_mlp)]:
        own_row, far_row = mine[...].astype(F32), other[...].astype(F32)
        table.append(jnp.where(first, own_row, far_row))
        table.append(jnp.where(first, far_row, own_row))
    for k, row in enumerate(table):
        gains[pl.ds(k, 1), :] = row
    normed[...] = norm_rows(hidden[...].astype(F32), table[0])
    each(units, "send")
    each(units, "forward")
    each(units, "arrive")
    copy = pltpu.make_async_copy(qkv_buf, qkv_out, out_sem)
    copy.start()
    each(units, "finish")
    copy.wait()


def attend_kernel(lens, normed, w_qkv, cos_t, sin_t, k_in, v_in, *rest, head_dim, aliased):
    if aliased:
        rest = rest[2:]
    k_out, v_out, attn_out, q_scr, k_scr, v_scr = rest
    batch = normed.shape[0]
    width = q_scr.shape[1]
    heads = width // head_dim
    half = head_dim // 2
    cache_len = k_in.shape[3]
    step = pl.program_id(0)

    @pl.when(step == 0)
    def _():
        proj = dot_nt(w_qkv[...], normed[...])
        cos_v, sin_v = cos_t[...], sin_t[...]

        def rope(block):
            pieces = []
            for head in range(heads):
                first = block[head * head_dim:head * head_dim + half]
                second = block[head * head_dim + half:(head + 1) * head_dim]
                pieces += [first * cos_v - second * sin_v, second * cos_v + first * sin_v]
            return jnp.concatenate(pieces, axis=0).astype(BF16).astype(F32)

        q_scr[...] = jnp.transpose(rope(proj[:width])) * (head_dim ** -0.5)
        pad = jnp.zeros((width, cache_len - batch), F32)
        k_scr[...] = jnp.concatenate([rope(proj[width:2 * width]), pad], axis=1)
        v_scr[...] = jnp.concatenate([proj[2 * width:].astype(BF16).astype(F32), pad], axis=1)

    seq0 = step * SEQ_TILE
    shift = lax.rem(cache_len - seq0, cache_len)
    k_cols = pltpu.roll(k_scr[...], shift, 1)
    v_cols = pltpu.roll(v_scr[...], shift, 1)
    lane = lax.broadcasted_iota(jnp.int32, (width, cache_len), 1)
    own_head = (lax.broadcasted_iota(jnp.int32, (HEAD_ROWS, width), 1) // head_dim
                == lax.broadcasted_iota(jnp.int32, (HEAD_ROWS, width), 0))
    lane_row = lax.broadcasted_iota(jnp.int32, (HEAD_ROWS, cache_len), 1)
    scores = []
    for j in range(SEQ_TILE):
        length = lens[seq0 + j]
        k_new = jnp.where(lane == length, k_cols[:, j:j + 1], k_in[0, j].astype(F32)).astype(BF16)
        k_out[0, j] = k_new
        q_block = jnp.where(own_head, q_scr[pl.ds(seq0 + j, 1), :], 0.0).astype(BF16)
        score = dot_nn(q_block, k_new)
        scores.append(jnp.where(lane_row <= length, score, MASK_FILL))
    score = jnp.concatenate(scores, axis=0)
    expo = jnp.exp(score - jnp.max(score, axis=-1, keepdims=True))
    probs = (expo / jnp.sum(expo, axis=-1, keepdims=True)).astype(BF16)
    outs = []
    for j in range(SEQ_TILE):
        length = lens[seq0 + j]
        v_new = jnp.where(lane == length, v_cols[:, j:j + 1], v_in[0, j].astype(F32)).astype(BF16)
        v_out[0, j] = v_new
        mixed = dot_nt(probs[j * HEAD_ROWS:(j + 1) * HEAD_ROWS], v_new)
        outs.append(jnp.sum(jnp.where(own_head, mixed, 0.0), axis=0, keepdims=True))
    attn_out[...] = jnp.concatenate(outs, axis=0).astype(BF16)


def attend(layer, lens, normed, w_qkv, cos_t, sin_t, k_cache, v_cache, prior, head_dim):
    layers, batch, width, cache_len = k_cache.shape
    tile = pl.BlockSpec((1, SEQ_TILE, width, cache_len), lambda i, *_: (layer, i, 0, 0))
    whole = lambda arr: pl.BlockSpec(arr.shape, lambda i, *_: (0,) * arr.ndim)
    aliased = prior is not None
    operands = [normed, w_qkv, cos_t, sin_t, k_cache, v_cache]
    in_specs = [whole(normed), whole(w_qkv), whole(cos_t), whole(sin_t), tile, tile]
    aliases = {}
    if aliased:
        operands += list(prior)
        in_specs += [ANY, ANY]
        aliases = {7: 0, 8: 1}
    flat = jax.ShapeDtypeStruct(k_cache.shape, BF16)
    return pl.pallas_call(
        functools.partial(attend_kernel, head_dim=head_dim, aliased=aliased),
        grid_spec=pltpu.PrefetchScalarGridSpec(
            num_scalar_prefetch=1, grid=(batch // SEQ_TILE,), in_specs=in_specs,
            out_specs=[tile, tile, pl.BlockSpec((SEQ_TILE, width), lambda i, *_: (i, 0))],
            scratch_shapes=[pltpu.VMEM((batch, width), F32), pltpu.VMEM((width, cache_len), F32),
                            pltpu.VMEM((width, cache_len), F32)]),
        out_shape=[flat, flat, jax.ShapeDtypeStruct((batch, width), BF16)],
        input_output_aliases=aliases,
        name=f"attend_{layer}",
    )(lens, *operands)


def first_layer_kernel(tg_size, sizes, attn, hidden, gains, w_qkv, w_o, w_gu, w_dn,
                       normed, h_out, gu0_out, qkv1, o1, gate1,
                       o_buf, gate_buf, up_buf, dn_buf, part, slots, mid, gu_sem, sum_send, sum_recv,
                       *sems):
    place = Place(tg_size)
    index = [0]

    def make(kind, layer, src_ref, buf):
        out = []
        for src, base, stride, count in row_blocks(kind, sizes):
            out.append(Gather(place, sems, index[0], layer, src_ref.at[pl.ds(src, count), :], buf,
                              base, stride, count))
            index[0] += 1
        return out

    o_u = make("o", 0, w_o, o_buf)
    gate_u = make("gate", 0, w_gu, gate_buf)
    up_u = make("up", 0, w_gu, up_buf)
    dn_u = make("dn", 0, w_dn, dn_buf)
    next_u = make("qkv", 1, w_qkv, qkv1) + make("o", 1, w_o, o1) + make("gate", 1, w_gu, gate1)
    every = o_u + gate_u + up_u + dn_u + next_u
    sum_o = SumOverTg(place, part.at[0], slots.at[0], mid, (sum_send.at[0], sum_recv.at[0]))
    sum_d = SumOverTg(place, part.at[1], slots.at[1], normed, (sum_send.at[1], sum_recv.at[1]))
    count = slots.shape[2]
    own = pl.ds(pl.multiple_of(place.tg * count, count), count)
    ffn = gate_buf.shape[0]

    place.barrier(True)
    each(every, "start")
    o_u[0].send()
    gate_u[0].send()
    o_u[0].forward()
    o_u[0].arrive()
    part[0] = dot_nn(attn[...], o_buf[...])
    sum_o.scatter_start()
    gate_u[1].send()
    gate_u[0].forward()
    up_u[0].send()
    gate_u[1].forward()
    h_mid = (hidden[own, :].astype(F32) + sum_o.total()).astype(BF16).astype(F32)
    sum_o.spread_start(norm_rows(h_mid, gains[2:3, :]))
    up_u[1].send()
    up_u[0].forward()
    sum_o.spread_finish()
    each(gate_u, "arrive")
    act_in = mid[...]
    gate = dot_nt(act_in, gate_buf[...])
    gate = jax.nn.silu(gate)
    dn_u[0].send()
    up_u[1].forward()
    each(up_u, "arrive")
    gate_out_copy = pltpu.make_async_copy(gate_buf, gu0_out.at[pl.ds(0, ffn), :], gu_sem.at[0])
    up_out_copy = pltpu.make_async_copy(up_buf, gu0_out.at[pl.ds(ffn, ffn), :], gu_sem.at[1])
    gate_out_copy.start()
    up_out_copy.start()
    act = (gate * dot_nt(act_in, up_buf[...])).astype(BF16)
    dn_u[1].send()
    each(next_u[:2], "send")
    each(dn_u, "forward")
    each(dn_u, "arrive")
    part[1] = dot_nn(act, dn_buf[...])
    sum_d.scatter_start()
    each(next_u[2:], "send")
    each(next_u[:2], "forward")
    h_new = (h_mid + sum_d.total()).astype(BF16)
    h_out[...] = h_new
    sum_d.spread_start(norm_rows(h_new.astype(F32), gains[1:2, :]))
    each(next_u[2:], "forward")
    sum_d.spread_finish()
    each(next_u, "arrive")
    each(every, "finish")
    gate_out_copy.wait()
    up_out_copy.wait()


def last_layer_kernel(tg_size, sizes, attn, h_in, gains, o1, gate1, w_gu, w_dn,
                      hidden_out, up1_out,
                      up_buf, dn_buf, part, slots, mid, up_sem, sum_send, sum_recv, *sems):
    place = Place(tg_size)
    index = [0]

    def make(kind, layer, src_ref, buf):
        out = []
        for src, base, stride, count in row_blocks(kind, sizes):
            out.append(Gather(place, sems, index[0], layer, src_ref.at[pl.ds(src, count), :], buf,
                              base, stride, count))
            index[0] += 1
        return out

    up_u = make("up", 1, w_gu, up_buf)
    dn_u = make("dn", 1, w_dn, dn_buf)
    every = up_u + dn_u
    sum_o = SumOverTg(place, part.at[0], slots.at[0], mid, (sum_send.at[0], sum_recv.at[0]))
    sum_d = SumOverTg(place, part.at[1], slots.at[1], hidden_out, (sum_send.at[1], sum_recv.at[1]))

    place.barrier(True)
    each(every, "start")
    part[0] = dot_nn(attn[...], o1[...])
    sum_o.scatter_start()
    each(up_u, "send")
    dn_u[0].send()
    up_u[0].forward()
    h_mid = (h_in[...].astype(F32) + sum_o.total()).astype(BF16).astype(F32)
    sum_o.spread_start(norm_rows(h_mid, gains[3:4, :]))
    dn_u[1].send()
    up_u[1].forward()
    sum_o.spread_finish()
    act_in = mid[...]
    gate = jax.nn.silu(dot_nt(act_in, gate1[...]))
    each(dn_u, "forward")
    each(up_u, "arrive")
    up_out_copy = pltpu.make_async_copy(up_buf, up1_out, up_sem)
    up_out_copy.start()
    act = (gate * dot_nt(act_in, up_buf[...])).astype(BF16)
    each(dn_u, "arrive")
    part[1] = dot_nn(act, dn_buf[...])
    sum_d.scatter_start()
    h_new = (h_mid + sum_d.total()).astype(BF16)
    sum_d.spread_start(h_new)
    each(every, "finish")
    up_out_copy.wait()
    sum_d.spread_finish()


def remote_params(collective_id):
    return pltpu.CompilerParams(collective_id=collective_id, has_side_effects=True,
                                vmem_limit_bytes=48 * 1024 * 1024)


def solution(mesh):
    merge = mesh.shape["grp"]
    tg_size = mesh.shape["tg"]
    cache_spec = P(None, ROW_AXES, None, "tg", None)
    in_specs = (P(ROW_AXES, None), P(ROW_AXES), cache_spec, cache_spec,
                P("pp", None), P("pp", TRAIN_AXES, None), P("pp", None, TRAIN_AXES),
                P("pp", None), P("pp", TRAIN_AXES, None), P("pp", None, TRAIN_AXES))
    out_specs = (P(ROW_AXES, None), cache_spec, cache_spec, P(None, "tg", None), P(None, "tg", None))

    def body(hidden_in, seq_lens, k_cache, v_cache, attn_gain, w_qkv, w_o, mlp_gain, w_gate_up, w_down):
        batch, dim = hidden_in.shape
        layers, _, cache_len, kv_loc, head_dim = k_cache.shape
        width = kv_loc * head_dim
        ffn_rows = w_gate_up.shape[1] // 2
        ffn = ffn_rows * merge
        sizes = (head_dim, ffn_rows, merge)
        quarter = batch // tg_size
        w_qkv, w_gate_up = w_qkv[0], w_gate_up[0]
        w_o_t, w_down_t = jnp.transpose(w_o[0]), jnp.transpose(w_down[0])
        flat = lambda cache: jnp.transpose(cache, (0, 1, 3, 4, 2)).reshape(layers, batch, width, cache_len)
        k_flat, v_flat = flat(k_cache), flat(v_cache)
        inv_freq = jnp.power(ROPE_THETA, -jnp.arange(0, head_dim, 2).astype(F32) / head_dim)
        angles = inv_freq[:, None] * seq_lens.astype(F32)[None, :]
        cos_t, sin_t = jnp.cos(angles), jnp.sin(angles)
        dma = pltpu.SemaphoreType.DMA
        sds = jax.ShapeDtypeStruct

        normed, gains, qkv0 = pl.pallas_call(
            functools.partial(first_kernel, tg_size, sizes),
            in_specs=[VMEM, VMEM, VMEM, ANY], out_specs=[VMEM, VMEM, ANY],
            out_shape=[sds((batch, dim), BF16), sds((4, dim), F32), sds((3 * width, dim), BF16)],
            scratch_shapes=[pltpu.VMEM((3 * width, dim), BF16), pltpu.VMEM((1, dim), BF16),
                            pltpu.VMEM((1, dim), BF16), dma((2,)), dma((2,)), dma(())] + gather_sems(3),
            compiler_params=remote_params(1), name="first",
        )(hidden_in, attn_gain, mlp_gain, w_qkv)

        k_out, v_out, attn = attend(0, seq_lens, normed, qkv0, cos_t, sin_t, k_flat, v_flat, None, head_dim)

        normed, h_own, gu0, qkv1, o1, gate1 = pl.pallas_call(
            functools.partial(first_layer_kernel, tg_size, sizes),
            in_specs=[VMEM, VMEM, VMEM, ANY, ANY, ANY, ANY],
            out_specs=[VMEM, VMEM, ANY, ANY, ANY, ANY],
            out_shape=[sds((batch, dim), BF16), sds((quarter, dim), BF16), sds((2 * ffn, dim), BF16),
                       sds((3 * width, dim), BF16), sds((width, dim), BF16), sds((ffn, dim), BF16)],
            scratch_shapes=[pltpu.VMEM((width, dim), BF16), pltpu.VMEM((ffn, dim), BF16),
                            pltpu.VMEM((ffn, dim), BF16), pltpu.VMEM((ffn, dim), BF16),
                            pltpu.VMEM((2, batch, dim), F32), pltpu.VMEM((2, tg_size - 1, quarter, dim), F32),
                            pltpu.VMEM((batch, dim), BF16), dma((2,)),
                            dma((2, 2, tg_size - 1)), dma((2, 2, tg_size - 1))] + gather_sems(13),
            compiler_params=remote_params(2), name="layer_0",
        )(attn, hidden_in, gains, w_qkv, w_o_t, w_gate_up, w_down_t)

        k_out, v_out, attn = attend(1, seq_lens, normed, qkv1, cos_t, sin_t, k_flat, v_flat,
                                    (k_out, v_out), head_dim)

        hidden, up1 = pl.pallas_call(
            functools.partial(last_layer_kernel, tg_size, sizes),
            in_specs=[VMEM, VMEM, VMEM, VMEM, VMEM, ANY, ANY],
            out_specs=[VMEM, ANY],
            out_shape=[sds((batch, dim), BF16), sds((ffn, dim), BF16)],
            scratch_shapes=[pltpu.VMEM((ffn, dim), BF16), pltpu.VMEM((ffn, dim), BF16),
                            pltpu.VMEM((2, batch, dim), F32), pltpu.VMEM((2, tg_size - 1, quarter, dim), F32),
                            pltpu.VMEM((batch, dim), BF16), dma(()),
                            dma((2, 2, tg_size - 1)), dma((2, 2, tg_size - 1))] + gather_sems(4),
            compiler_params=remote_params(3), name="layer_1",
        )(attn, h_own, gains, o1, gate1, w_gate_up, w_down_t)

        unflat = lambda cache: jnp.transpose(
            cache.reshape(layers, batch, kv_loc, head_dim, cache_len), (0, 1, 4, 2, 3))
        gen_qkv = jnp.stack([qkv0, qkv1])
        gen_gate_up = jnp.stack([gu0, jnp.concatenate([gate1, up1], axis=0)])
        return hidden, unflat(k_out), unflat(v_out), gen_qkv, gen_gate_up

    return jax.shard_map(body, mesh=mesh, in_specs=in_specs, out_specs=out_specs, check_vma=False)
```

time: 498 us -> 158 us (0.32)
  waiting for transfers between devices: 254 us -> 0 us
  local copies, waits for them, and re-layouts: 164 us -> 11.4 us
  Pallas kernels: 0 us -> 139 us
  matrix products: 35.8 us -> 0 us
  blocking collectives: 16.1 us -> 0 us
  between operations: 14.2 us -> 0.77 us
    all_gather x7 -> x0, waiting for transfers between devices: 147 us -> none  [the longest x1 75.2 us: regroup_weights(): lax.all_gather(gate_up.reshape(1, -1, model_dim), 'pp', axis=0, tiled=True)]
    pallas_call x0 -> x5, Pallas kernels: none -> 139 us  [the longest x1 55.6 us: body(): pl.pallas_call(functools.partial(first_layer_kernel, tg_size, sizes), in_...]
    psum x4 -> x0, waiting for transfers between devices: 105 us -> none  [body(): lax.psum(tp_part, 'tg')]
    unnamed x20 -> x41, local copies, waits for them, and re-layouts: 102 us -> 11.4 us
    dot_general x12 -> x0, matrix products: 35.8 us -> none  [the longest x2 12.9 us: attend(): jnp.einsum('bgrd,bsgd->bgrs', query_vals, k_layer, preferred_element_type...]
    scatter x4 -> x0, local copies, waits for them, and re-layouts: 32.1 us -> none  [the longest x2 16.1 us: body(): v_cache = v_cache.at[layer_idx, row_ids, seq_lens].set(value_new)]
    squeeze x4 -> x0, local copies, waits for them, and re-layouts: 24.2 us -> none  [the longest x2 13.4 us: body(): k_cache[layer_idx]]
    all_gather x3 -> x0, blocking collectives: 16.1 us -> none  [the longest x1 7.16 us: regroup_weights(): lax.all_gather(w_o, 'grp', axis=2, tiled=True)]
  transfers between devices with their start and end apart: 11 -> 0, of which waited for: 7 -> 0; matrix products, arithmetic and copies ran while one was open for 29% -> 0% of each run, Pallas kernels for 0% -> 0%
where the time goes in v1:
time: 158 us
  Pallas kernels  139 us (88%)
  local copies, waits for them, and re-layouts  11.4 us (7%)
  other arithmetic  6.66 us (4%)
    pallas_call x1, Pallas kernels, body(): pl.pallas_call(functools.partial(first_layer_kernel, tg_size, sizes), in_...  55.6 us
    pallas_call x1, Pallas kernels, body(): pl.pallas_call(functools.partial(last_layer_kernel, tg_size, sizes), in_s...  44.7 us
    pallas_call x2, Pallas kernels, attend(): pl.pallas_call(functools.partial(attend_kernel, head_dim=head_dim, aliase...  22 us
    pallas_call x1, Pallas kernels, body(): pl.pallas_call(functools.partial(first_kernel, tg_size, sizes), in_specs=...  16.5 us
    unnamed x41, local copies, waits for them, and re-layouts  11.4 us
    another operation x2, other arithmetic, body(): gen_gate_up = jnp.stack([gu0, jnp.concatenate([gate1, up1], axis=0)])  3.3 us

profile of v1, /device:TPU:0, one launch (start us, length us, event | category | flops | bytes accessed | tf_op | source)
XLA Modules:
  0.0 157.6 jit_solution(3667699855873464252)
XLA Ops:
  0.6 0.7 convert_element_type.11
  1.3 0.8 multiply_sine_fusion
  2.1 0.0 copy-start.5
  2.1 1.0 copy-done.5
  3.0 0.0 copy-start.8
  3.0 0.9 copy-done.8
  4.0 0.0 copy-start.17
  4.0 0.7 copy-done.17
  4.6 0.0 copy-start.18
  4.6 0.7 copy-done.18
  5.3 16.5 %first.1 = (bf16[64,1024]{1,0:T(8,128)(2,1)S(1)}, f32[4,1024]{1,0:T(4,128)S(1)}, bf16[768,1024]{1,0:T(8,128)(2,1)S(1)}) custom-call(bf16[64,1024]{1,0:T(8,128)(2,1)S(1)} %copy-done.8, bf16[1,1024]{1,0:T(2,128)(2,1)S(1)} %copy-done.17, bf16[1,1024]{1,0:T(2,128)(2,1)S(1)} %copy-done.18, bf16[192,1024]{1,0:T(8,128)(2,1)S(1)} %bitcast.29), custom_call_target="tpu_custom_call" | custom-call | tf_op jit(solution)/shard_map/first/pallas_call | solution.py:487
  21.8 0.0 copy-start.2
  21.8 1.1 copy-done.2
  22.9 0.0 copy-start.13
  22.9 0.7 copy-done.13
  23.6 0.0 copy-start.4
  23.6 0.0 copy-start.6
  23.6 0.0 copy-start.7
  23.6 0.0 copy-start.9
  23.6 0.0 copy-start.14
  23.6 11.0 %attend_0.1 = (bf16[2,64,256,128]{3,2,1,0:T(8,128)(2,1)}, bf16[2,64,256,128]{3,2,1,0:T(8,128)(2,1)}, bf16[64,256]{1,0:T(8,128)(2,1)}) custom-call(s32[64]{0:T(128)} %lens.3, bf16[64,1024]{1,0:T(8,128)(2,1)} %copy-done.13, bf16[768,1024]{1,0:T(8,128)(2,1)} %copy-done.2, f32[32,64]{1,0:T(8,128)} %get-tuple-element.40.cos_t, f32[32,64]{1,0:T(8,128)} %get-tuple-element.39.sin_t, ...), custom_call_target="tpu_custom_call" | custom-call | tf_op jit(solution)/shard_map/attend_0/pallas_call | solution.py:318
  34.6 0.0 copy-done.4
  34.6 0.0 copy-done.6
  34.6 0.0 copy-done.7
  34.6 0.0 copy-done.9
  34.6 0.0 copy-done.14
  34.7 0.0 copy-start.16
  34.7 0.7 copy-done.16
  35.4 55.6 %layer_0.1 = (bf16[64,1024]{1,0:T(8,128)(2,1)S(1)}, bf16[16,1024]{1,0:T(8,128)(2,1)S(1)}, bf16[1408,1024]{1,0:T(8,128)(2,1)}, bf16[768,1024]{1,0:T(8,128)(2,1)S(...) custom-call(bf16[64,256]{1,0:T(8,128)(2,1)S(1)} %copy-done.16, bf16[64,1024]{1,0:T(8,128)(2,1)S(1)} %copy-done.9, ...), custom_call_target="tpu_custom_call" | custom-call | tf_op jit(solution)/shard_map/layer_0/pallas_call | solution.py:498
  91.0 0.0 copy-start
  91.0 1.1 copy-done
  92.2 0.0 copy-start.10
  92.2 0.8 copy-done.10
  93.0 0.0 copy-start.12
  93.0 0.7 copy-done.12
  93.6 0.0 copy-start.11
  93.6 11.0 %attend_1.1 = (bf16[2,64,256,128]{3,2,1,0:T(8,128)(2,1)}, bf16[2,64,256,128]{3,2,1,0:T(8,128)(2,1)}, bf16[64,256]{1,0:T(8,128)(2,1)}) custom-call(s32[64]{0:T(128)} %lens.3, bf16[64,1024]{1,0:T(8,128)(2,1)} %copy-done.12, bf16[768,1024]{1,0:T(8,128)(2,1)} %copy-done, ...), custom_call_target="tpu_custom_call", output_to_operand_aliasing={{0}: (7, {}), {1}: (8, {})} | custom-call | tf_op jit(solution)/shard_map/attend_1/pallas_call | solution.py:318
  104.6 0.0 copy-done.11
  104.6 0.0 copy-start.15
  104.7 0.7 copy-done.15
  105.4 44.7 %layer_1.1 = (bf16[64,1024]{1,0:T(8,128)(2,1)S(1)}, bf16[704,1024]{1,0:T(8,128)(2,1)S(1)}) custom-call(bf16[64,256]{1,0:T(8,128)(2,1)S(1)} %copy-done.15, bf16[16,1024]{1,0:T(8,128)(2,1)S(1)} %get-tuple-element.31.h_in, f32[4,1024]{1,0:T(4,128)S(1)} %get-tuple-element.25.gains, bf16[256,1024]{1,0:T(8,128)(2,1)S(1)} %copy-done.11, ...), custom_call_target="tpu_custom_call" | custom-call | tf_op jit(solution)/shard_map/layer_1/pallas_call | solution.py:515
  150.1 0.0 copy-start.19
  150.1 0.3 maximum_bitcast_fusion
  150.4 1.5 copy-done.19
  151.9 0.0 copy-start.1
  151.9 0.0 copy-start.3
  151.9 3.0 %pad_maximum_fusion = bf16[2,1408,1024]{2,1,0:T(8,128)(2,1)} fusion(bf16[1,1408,1024]{2,1,0:T(8,128)(2,1)S(1)} %maximum_bitcast_fusion, bf16[1,1408,1024]{2,1,0:T(8,128)(2,1)S(1)} %bitcast.40), kind=kLoop, calls=%fused_computation | loop fusion | flops 2883584 | bytes 11534336 | tf_op jit(solution)/shard_map/stack | solution.py:530
  155.0 0.0 copy-done.1
  155.0 0.0 copy-done.3
  155.0 1.9 %pad_maximum_fusion.1 = bf16[2,768,1024]{2,1,0:T(8,128)(2,1)} fusion(bf16[1,768,1024]{2,1,0:T(8,128)(2,1)S(1)} %bitcast.25, bf16[1,768,1024]{2,1,0:T(8,128)(2,1)S(1)} %bitcast.26), kind=kLoop, calls=%fused_computation.1 | loop fusion | flops 1572864 | bytes 6291456 | tf_op jit(solution)/shard_map/stack | solution.py:529
  156.9 0.7 copy.20
  (1 shorter events, 0.0 us)
Async XLA Ops:
  2.1 1.0 copy-start.5
  3.0 0.9 copy-start.8
  4.0 0.7 copy-start.17
  4.6 0.7 copy-start.18
  21.8 1.1 copy-start.2
  22.9 0.7 copy-start.13
  23.6 11.0 %copy-start.4 = (bf16[1,352,1024]{2,1,0:T(8,128)(2,1)S(1)}, bf16[1,352,1024]{2,1,0:T(8,128)(2,1)}, u32[]{:S(2)}) copy-start(bf16[1,352,1024]{2,1,0:T(8,128)(2,1)} %param.18) | copy-start | bytes 2162692
  23.6 11.0 %copy-start.6 = (bf16[1,192,1024]{2,1,0:T(8,128)(2,1)S(1)}, bf16[1,192,1024]{2,1,0:T(8,128)(2,1)}, u32[]{:S(2)}) copy-start(bf16[1,192,1024]{2,1,0:T(8,128)(2,1)} %param.15) | copy-start | bytes 1179652
  23.6 11.0 %copy-start.7 = (bf16[1,1024,176]{1,2,0:T(8,128)(2,1)S(1)}, bf16[1,1024,176]{1,2,0:T(8,128)(2,1)}, u32[]{:S(2)}) copy-start(bf16[1,1024,176]{1,2,0:T(8,128)(2,1)} %param.19) | copy-start | bytes 1081348
  23.6 11.0 %copy-start.9 = (bf16[64,1024]{1,0:T(8,128)(2,1)S(1)}, bf16[64,1024]{1,0:T(8,128)(2,1)}, u32[]{:S(2)}) copy-start(bf16[64,1024]{1,0:T(8,128)(2,1)} %hidden.3) | copy-start | bytes 393220
  23.6 11.0 %copy-start.14 = (bf16[1,1024,64]{1,2,0:T(8,128)(2,1)S(1)}, bf16[1,1024,64]{1,2,0:T(8,128)(2,1)}, u32[]{:S(2)}) copy-start(bf16[1,1024,64]{1,2,0:T(8,128)(2,1)} %param.16) | copy-start | bytes 393220
  34.7 0.8 copy-start.16
  91.0 1.2 copy-start
  92.2 0.8 copy-start.10
  93.0 0.7 copy-start.12
  93.6 11.0 %copy-start.11 = (bf16[256,1024]{1,0:T(8,128)(2,1)S(1)}, bf16[256,1024]{1,0:T(8,128)(2,1)}, u32[]{:S(2)}) copy-start(bf16[256,1024]{1,0:T(8,128)(2,1)} %copy-done.10) | copy-start | bytes 1572868
  104.6 0.8 copy-start.15
  150.1 1.8 %copy-start.19 = (bf16[1408,1024]{1,0:T(8,128)(2,1)S(1)}, bf16[1408,1024]{1,0:T(8,128)(2,1)}, u32[]{:S(2)}) copy-start(bf16[1408,1024]{1,0:T(8,128)(2,1)} %get-tuple-element.37) | copy-start | bytes 8650756
  151.9 3.0 %copy-start.1 = (bf16[768,1024]{1,0:T(8,128)(2,1)S(1)}, bf16[768,1024]{1,0:T(8,128)(2,1)}, u32[]{:S(2)}) copy-start(bf16[768,1024]{1,0:T(8,128)(2,1)} %copy-done) | copy-start | bytes 4718596
  151.9 3.0 %copy-start.3 = (bf16[768,1024]{1,0:T(8,128)(2,1)S(1)}, bf16[768,1024]{1,0:T(8,128)(2,1)}, u32[]{:S(2)}) copy-start(bf16[768,1024]{1,0:T(8,128)(2,1)} %copy-done.2) | copy-start | bytes 4718596

commit v2 on v1

v2 whole, which is shorter than its diff:
```python
import functools
import math

import jax
import jax.numpy as jnp
from jax import lax
from jax.experimental import pallas as pl
from jax.experimental.pallas import tpu as pltpu
from jax.sharding import PartitionSpec as P

ROPE_THETA = 500000.0
NORM_EPS = 1e-5
MASK_FILL = -1e30
ROW_AXES = ("pp", "grp")
TRAIN_AXES = ("tg", "grp")
BF16 = jnp.bfloat16
F32 = jnp.float32
MESH = pl.DeviceIdType.MESH
HBM = pl.BlockSpec(memory_space=pltpu.HBM)
SMEM = pl.BlockSpec(memory_space=pltpu.SMEM)
VMEM = pl.BlockSpec(memory_space=pltpu.VMEM)
SEQ_TILE = 16
HEAD_ROWS = 8


def norm_rows(hidden_f32, gain_row):
    inv_rms = lax.rsqrt(jnp.mean(hidden_f32 * hidden_f32, axis=-1, keepdims=True) + NORM_EPS)
    return (hidden_f32 * inv_rms * gain_row).astype(BF16)


def rows(ref, start, count):
    return ref.at[pl.ds(pl.multiple_of(start, 16), count), :]


class Place:
    def __init__(self, tg_size):
        self.tg_size = tg_size
        self.tg = lax.axis_index("tg")
        self.pp = lax.axis_index("pp")
        self.grp = lax.axis_index("grp")
        self.partner = self.grp + 1 - 2 * lax.rem(self.grp, 2)
        self.across = lax.rem(self.grp + 2, 4)
        self.diagonal = lax.rem(self.partner + 2, 4)
        self.stage = 1 - self.pp

    def tg_at(self, step):
        return lax.rem(self.tg + step, self.tg_size)

    def barrier(self, with_tg):
        sem = pltpu.get_barrier_semaphore()
        targets = [{"grp": self.partner}, {"grp": self.across}, {"pp": self.stage}]
        if with_tg:
            targets += [{"tg": self.tg_at(step)} for step in range(1, self.tg_size)]
        for target in targets:
            pl.semaphore_signal(sem, inc=1, device_id=target, device_id_type=MESH)
        pl.semaphore_wait(sem, len(targets))


def gather_sems(count):
    dma = pltpu.SemaphoreType.DMA
    return [dma((count,)), dma((count, 2)), dma((count, 2)), dma((count, 2)), dma((count, 2, 2))]


class Cross:
    def __init__(self, place, sems, index, layer, own, held):
        self.place, self.layer = place, layer
        self.copy = lambda: pltpu.make_async_remote_copy(
            src_ref=own, dst_ref=held, send_sem=sems[1].at[index, 0], recv_sem=sems[1].at[index, 1],
            device_id={"pp": place.stage}, device_id_type=MESH)

    def start(self):
        @pl.when(self.place.pp == self.layer)
        def _():
            self.copy().start()

    def finish(self):
        @pl.when(self.place.pp == self.layer)
        def _():
            self.copy().wait_send()

        @pl.when(self.place.pp != self.layer)
        def _():
            self.copy().wait_recv()


class Gather:
    def __init__(self, place, sems, index, layer, own, held, buf, base, stride, count, route):
        self.place, self.layer, self.own, self.held, self.buf = place, layer, own, held, buf
        self.base, self.stride, self.count, self.route = base, stride, count, route
        local, ysem, zsem, xsem, psem = sems
        self.local = local.at[index]
        self.ysem = (ysem.at[index, 0], ysem.at[index, 1])
        self.zsem = (zsem.at[index, 0], zsem.at[index, 1])
        self.xsem = (xsem.at[index, 0], xsem.at[index, 1])
        self.psem = [(psem.at[index, k, 0], psem.at[index, k, 1]) for k in range(2)]

    def on(self, owner, body):
        pl.when(self.place.pp == self.layer if owner else self.place.pp != self.layer)(body)

    def at(self, grp):
        return rows(self.buf, self.base + grp * self.stride, self.count)

    def remote(self, src, grp, sems, target):
        return pltpu.make_async_remote_copy(
            src_ref=src, dst_ref=self.at(grp), send_sem=sems[0], recv_sem=sems[1],
            device_id=target, device_id_type=MESH)

    def local_copy(self, src):
        return pltpu.make_async_copy(src, self.at(self.place.grp), self.local)

    def y_copy(self):
        return self.remote(self.own, self.place.grp, self.ysem, {"pp": self.place.stage})

    def z_copy(self):
        grp = self.place.across
        return self.remote(self.at(grp), grp, self.zsem, {"pp": self.place.stage})

    def x_copy(self, grp):
        return self.remote(self.at(grp), grp, self.xsem, {"grp": self.place.across})

    def p_copy(self, grp, which):
        return self.remote(self.at(grp), grp, self.psem[which], {"grp": self.place.partner})

    def start(self):
        def owner():
            if self.held is None:
                self.y_copy().start()
            self.local_copy(self.own).start()

        self.on(True, owner)
        if self.held is not None:
            self.on(False, lambda: self.local_copy(self.held).start())

    def send(self):
        self.on(True, lambda: self.local_copy(self.own).wait())
        if self.held is None:
            self.on(False, lambda: self.y_copy().wait_recv())
        else:
            self.on(False, lambda: self.local_copy(self.held).wait())
        grp = self.place.grp
        if self.route == "both":
            self.x_copy(grp).start()
        else:
            self.on(self.route == "owner", lambda: self.x_copy(grp).start())
        self.p_copy(grp, 0).start()

    def forward(self):
        grp = self.place.across
        if self.route == "both":
            self.x_copy(grp).wait_recv()
        else:
            def relay():
                self.x_copy(grp).wait_recv()
                self.z_copy().start()

            self.on(self.route == "owner", relay)
            self.on(self.route != "owner", lambda: self.z_copy().wait_recv())
        self.p_copy(grp, 1).start()

    def arrive(self):
        self.p_copy(self.place.partner, 0).wait_recv()
        self.p_copy(self.place.diagonal, 1).wait_recv()

    def finish(self):
        if self.held is None:
            self.on(True, lambda: self.y_copy().wait_send())
        grp = self.place.grp
        if self.route == "both":
            self.x_copy(grp).wait_send()
        else:
            def relayed():
                self.x_copy(grp).wait_send()
                self.z_copy().wait_send()

            self.on(self.route == "owner", relayed)
        self.p_copy(grp, 0).wait_send()
        self.p_copy(self.place.across, 1).wait_send()


class Maker:
    def __init__(self, place, sems, sizes):
        self.place, self.sems, self.sizes, self.index = place, sems, sizes, 0

    def gather(self, kind, layer, src_ref, buf, routes, held=None):
        out = []
        for (src, hold, base, stride, count), route in zip(row_blocks(kind, self.sizes), routes, strict=True):
            out.append(Gather(self.place, self.sems, self.index, layer, src_ref.at[pl.ds(src, count), :],
                              None if held is None else held.at[pl.ds(hold, count), :],
                              buf, base, stride, count, route))
            self.index += 1
        return out

    def cross(self, kind, layer, src_ref, held):
        out = []
        for src, hold, _, _, count in row_blocks(kind, self.sizes):
            out.append(Cross(self.place, self.sems, self.index, layer, src_ref.at[pl.ds(src, count), :],
                             held.at[pl.ds(hold, count), :]))
            self.index += 1
        return out


def each(units, what):
    for unit in units:
        getattr(unit, what)()


def row_blocks(kind, sizes):
    head_rows, ffn_rows, merge = sizes
    top = (ffn_rows // 2 + 15) // 16 * 16
    halves = [(0, top), (top, ffn_rows - top)]
    if kind == "qkv":
        return [(k * head_rows, k * head_rows, k * merge * head_rows, head_rows, head_rows) for k in range(3)]
    if kind == "o":
        return [(0, 0, 0, head_rows, head_rows)]
    shift = ffn_rows if kind == "up" else 0
    return [(shift + off, off, off, ffn_rows, count) for off, count in halves]


class SumOverTg:
    def __init__(self, place, part, slots, full, sems):
        self.place, self.part, self.slots, self.full = place, part, slots, full
        self.count = slots.shape[1]
        self.send, self.recv = sems

    def scatter_copy(self, step):
        peer = self.place.tg_at(step)
        return pltpu.make_async_remote_copy(
            src_ref=rows(self.part, peer * self.count, self.count), dst_ref=self.slots.at[step - 1],
            send_sem=self.send.at[0, step - 1], recv_sem=self.recv.at[0, step - 1],
            device_id={"tg": peer}, device_id_type=MESH)

    def spread_copy(self, step):
        own = rows(self.full, self.place.tg * self.count, self.count)
        return pltpu.make_async_remote_copy(
            src_ref=own, dst_ref=own,
            send_sem=self.send.at[1, step - 1], recv_sem=self.recv.at[1, step - 1],
            device_id={"tg": self.place.tg_at(step)}, device_id_type=MESH)

    def spread_wait(self, step):
        peer = self.place.tg_at(self.place.tg_size - step)
        block = rows(self.full, peer * self.count, self.count)
        pltpu.make_async_remote_copy(
            src_ref=block, dst_ref=block,
            send_sem=self.send.at[1, step - 1], recv_sem=self.recv.at[1, step - 1],
            device_id={"tg": peer}, device_id_type=MESH).wait_recv()

    def steps(self):
        return range(1, self.place.tg_size)

    def far_first(self):
        return (2, 3, 1) if self.place.tg_size == 4 else self.steps()

    def scatter_start(self):
        for step in self.far_first():
            self.scatter_copy(step).start()

    def total(self):
        for step in self.steps():
            self.scatter_copy(step).wait_recv()
        out = self.part[pl.ds(pl.multiple_of(self.place.tg * self.count, self.count), self.count), :]
        for step in self.steps():
            out = out + self.slots[step - 1]
        return out

    def spread_start(self, block):
        self.full[pl.ds(pl.multiple_of(self.place.tg * self.count, self.count), self.count), :] = block
        for step in self.steps():
            self.scatter_copy(step).wait_send()
        for step in self.far_first():
            self.spread_copy(step).start()

    def spread_finish(self):
        for step in self.steps():
            self.spread_wait(step)
        for step in self.steps():
            self.spread_copy(step).wait_send()


def dot_nt(lhs, rhs):
    return lax.dot_general(lhs, rhs, (((1,), (1,)), ((), ())), preferred_element_type=F32)


def dot_nn(lhs, rhs):
    return jnp.dot(lhs, rhs, preferred_element_type=F32)


BOTH2, HALVES = ("both", "both"), ("owner", "other")


def first_kernel(tg_size, sizes, layers, hidden, lens, attn_gain, mlp_gain, w_qkv, w_o, w_gu, k_cache, v_cache,
                 normed, gains, cos_t, sin_t, qkv0, o0, k_next, v_next, gate_held,
                 hidden_buf, own_gain, far_gain, load_sem, gain_send, gain_recv, *sems):
    place = Place(tg_size)
    make = Maker(place, sems, sizes)
    units = make.gather("qkv", 0, w_qkv, qkv0, ("both",) * 3) + make.gather("o", 0, w_o, o0, ("both",))
    gate_piece = make.cross("gate", 0, w_gu, gate_held) + make.cross("gate", 1, w_gu, gate_held)
    loads = [pltpu.make_async_copy(src, dst, load_sem.at[k]) for k, (src, dst) in enumerate([
        (hidden, hidden_buf), (attn_gain, own_gain.at[0]), (mlp_gain, own_gain.at[1]),
        (k_cache.at[0], k_next), (v_cache.at[0], v_next)])]
    for copy in loads[:3]:
        copy.start()
    place.barrier(False)
    each(units, "start")
    for copy in loads[3:]:
        copy.start()
    for copy in loads[1:3]:
        copy.wait()
    gain_copies = [
        pltpu.make_async_remote_copy(
            src_ref=own_gain.at[k], dst_ref=far_gain.at[k], send_sem=gain_send.at[k], recv_sem=gain_recv.at[k],
            device_id={"pp": place.stage}, device_id_type=MESH) for k in range(2)]
    for copy in gain_copies:
        copy.start()
    each(gate_piece, "start")
    half = cos_t.shape[0]
    power = lax.broadcasted_iota(jnp.int32, cos_t.shape, 0).astype(F32) * (-math.log(ROPE_THETA) / half)
    angle = jnp.exp(power) * lens[...].astype(F32)
    cos_t[...] = jnp.cos(angle)
    sin_t[...] = jnp.sin(angle)
    each(units[:1], "send")
    for copy in gain_copies:
        copy.wait()
    loads[0].wait()
    first = place.pp == 0
    table = []
    for k in range(2):
        own_row, far_row = own_gain[k].astype(F32), far_gain[k].astype(F32)
        table.append(jnp.where(first, own_row, far_row))
        table.append(jnp.where(first, far_row, own_row))
    for k, row in enumerate(table):
        gains[pl.ds(k, 1), :] = row
    normed[...] = norm_rows(hidden_buf[...].astype(F32), table[0])
    each(units[1:2], "send")
    each(units[:1], "forward")
    each(units[2:3], "send")
    each(units[1:2], "forward")
    each(units[3:], "send")
    each(units[2:], "forward")
    each(units, "arrive")
    each(units, "finish")
    for copy in loads[3:]:
        copy.wait()
    each(gate_piece, "finish")


def attend_kernel(layer, head_dim, rest_in, lens, normed, w_qkv, cos_t, sin_t, k_in, v_in, *rest):
    rest = rest[rest_in:] if not layer else rest
    if layer:
        gate, up = rest[:2]
        rest = rest[2 + rest_in:]
        k_out, v_out, gen_qkv, gen_gu, attn_out = rest[:5]
        rest = rest[5:]
    else:
        k_out, v_out, gen_qkv, attn_out = rest[:4]
        rest = rest[4:]
    k_new, v_new, q_scr, k_scr, v_scr, kv_sem, gen_sem = rest
    gens = [pltpu.make_async_copy(w_qkv, gen_qkv.at[layer], gen_sem.at[0])]
    if layer:
        ffn = gate.shape[0]
        gens += [pltpu.make_async_copy(gate, gen_gu.at[0, pl.ds(0, ffn)], gen_sem.at[1]),
                 pltpu.make_async_copy(up, gen_gu.at[0, pl.ds(ffn, ffn)], gen_sem.at[2])]
    for copy in gens:
        copy.start()
    batch = normed.shape[0]
    width = q_scr.shape[1]
    heads = width // head_dim
    half = head_dim // 2
    cache_len = k_in.shape[2]
    proj = dot_nt(w_qkv[...], normed[...])
    cos_v, sin_v = cos_t[...], sin_t[...]

    def rope(block):
        pieces = []
        for head in range(heads):
            first = block[head * head_dim:head * head_dim + half]
            second = block[head * head_dim + half:(head + 1) * head_dim]
            pieces += [first * cos_v - second * sin_v, second * cos_v + first * sin_v]
        return jnp.concatenate(pieces, axis=0).astype(BF16).astype(F32)

    q_scr[...] = jnp.transpose(rope(proj[:width])) * (head_dim ** -0.5)
    pad = jnp.zeros((width, cache_len - batch), F32)
    k_scr[...] = jnp.concatenate([rope(proj[width:2 * width]), pad], axis=1)
    v_scr[...] = jnp.concatenate([proj[2 * width:].astype(BF16).astype(F32), pad], axis=1)
    lane = lax.broadcasted_iota(jnp.int32, (width, cache_len), 1)
    own_head = (lax.broadcasted_iota(jnp.int32, (HEAD_ROWS, width), 1) // head_dim
                == lax.broadcasted_iota(jnp.int32, (HEAD_ROWS, width), 0))
    lane_row = lax.broadcasted_iota(jnp.int32, (HEAD_ROWS, cache_len), 1)

    def copy_out(k, i):
        block = pl.ds(i * SEQ_TILE, SEQ_TILE)
        new, out = [(k_new, k_out), (v_new, v_out)][k]
        return pltpu.make_async_copy(new.at[block], out.at[layer, block], kv_sem.at[k, i])

    def placed(length, seq, cols, old):
        moved = pltpu.roll(cols, lax.rem(length - seq + cache_len, cache_len), 1).astype(BF16)
        return jnp.where(lane == length, moved, old)

    def step(i, carry):
        seq0 = i * SEQ_TILE
        k_cols, v_cols = k_scr[...], v_scr[...]
        scores = []
        for j in range(SEQ_TILE):
            length = lens[seq0 + j]
            k_val = placed(length, seq0 + j, k_cols, k_in[seq0 + j])
            k_new[seq0 + j] = k_val
            q_block = jnp.where(own_head, q_scr[pl.ds(seq0 + j, 1), :], 0.0).astype(BF16)
            scores.append(jnp.where(lane_row <= length, dot_nn(q_block, k_val), MASK_FILL))
        copy_out(0, i).start()
        score = jnp.concatenate(scores, axis=0)
        expo = jnp.exp(score - jnp.max(score, axis=-1, keepdims=True))
        probs = (expo / jnp.sum(expo, axis=-1, keepdims=True)).astype(BF16)
        outs = []
        for j in range(SEQ_TILE):
            v_val = placed(lens[seq0 + j], seq0 + j, v_cols, v_in[seq0 + j])
            v_new[seq0 + j] = v_val
            mixed = dot_nt(probs[j * HEAD_ROWS:(j + 1) * HEAD_ROWS], v_val)
            outs.append(jnp.sum(jnp.where(own_head, mixed, 0.0), axis=0, keepdims=True))
        copy_out(1, i).start()
        attn_out[pl.ds(pl.multiple_of(seq0, SEQ_TILE), SEQ_TILE), :] = jnp.concatenate(outs, axis=0).astype(BF16)
        return carry

    steps = batch // SEQ_TILE
    lax.fori_loop(0, steps, step, 0)
    for i in range(steps):
        copy_out(0, i).wait()
        copy_out(1, i).wait()
    for copy in gens:
        copy.wait()


def attend(layer, lens, normed, w_qkv, cos_t, sin_t, k_now, v_now, head_dim, layers, extra=(), prior=()):
    batch, width, cache_len = k_now.shape
    sds = jax.ShapeDtypeStruct
    flat = sds((layers,) + k_now.shape, BF16)
    gen = [sds((layers,) + w_qkv.shape, BF16)]
    if layer:
        gen.append(sds((layers, 2 * extra[0].shape[0], extra[0].shape[1]), BF16))
    return pl.pallas_call(
        functools.partial(attend_kernel, layer, head_dim, len(prior)),
        in_specs=[SMEM] + [VMEM] * (6 + len(extra)) + [HBM] * len(prior),
        out_specs=[HBM, HBM] + [HBM] * len(gen) + [VMEM],
        out_shape=[flat, flat] + gen + [sds((batch, width), BF16)],
        scratch_shapes=[pltpu.VMEM(k_now.shape, BF16)] * 2 + [
            pltpu.VMEM((batch, width), F32), pltpu.VMEM((width, cache_len), F32),
            pltpu.VMEM((width, cache_len), F32), pltpu.SemaphoreType.DMA((2, batch // SEQ_TILE)),
            pltpu.SemaphoreType.DMA((3,))],
        input_output_aliases={7 + len(extra) + k: k for k in range(len(prior))},
        compiler_params=pltpu.CompilerParams(vmem_limit_bytes=32 * 1024 * 1024),
        name=f"attend_{layer}",
    )(lens, normed, w_qkv, cos_t, sin_t, k_now, v_now, *extra, *prior)


def first_layer_kernel(tg_size, sizes, attn, hidden, gains, o0, gate_held, w_qkv, w_o, w_gu, w_dn, k_cache, v_cache,
                       normed, h_out, gate_buf, up_buf, qkv1, o1, k_next, v_next, up_held, dn_held,
                       dn_buf, part, slots, mid, h_own, load_sem, sum_send, sum_recv, *sems):
    place = Place(tg_size)
    make = Maker(place, sems, sizes)
    gate_u = make.gather("gate", 0, w_gu, gate_buf, BOTH2, gate_held)
    up_u = make.gather("up", 0, w_gu, up_buf, BOTH2)
    dn_u = make.gather("dn", 0, w_dn, dn_buf, ("both", "owner"))
    next_u = make.gather("qkv", 1, w_qkv, qkv1, ("both",) * 3) + make.gather("o", 1, w_o, o1, ("both",))
    crossing = make.cross("up", 1, w_gu, up_held) + make.cross("dn", 1, w_dn, dn_held)
    every = gate_u + up_u + dn_u + next_u
    sum_o = SumOverTg(place, part.at[0], slots.at[0], mid, (sum_send.at[0], sum_recv.at[0]))
    sum_d = SumOverTg(place, part.at[1], slots.at[1], normed, (sum_send.at[1], sum_recv.at[1]))
    count = slots.shape[2]
    loads = [pltpu.make_async_copy(src, dst, load_sem.at[k]) for k, (src, dst) in enumerate([
        (rows(hidden, place.tg * count, count), h_own), (k_cache.at[1], k_next), (v_cache.at[1], v_next)])]

    loads[0].start()
    place.barrier(True)
    each(every, "start")
    part[0] = dot_nn(attn[...], o0[...])
    sum_o.scatter_start()
    each(crossing, "start")
    each(gate_u, "send")
    for copy in loads[1:]:
        copy.start()
    gate_u[0].forward()
    up_u[0].send()
    gate_u[1].forward()
    loads[0].wait()
    h_mid = (h_own[...].astype(F32) + sum_o.total()).astype(BF16).astype(F32)
    sum_o.spread_start(norm_rows(h_mid, gains[2:3, :]))
    up_u[1].send()
    up_u[0].forward()
    dn_u[0].send()
    sum_o.spread_finish()
    each(gate_u, "arrive")
    act_in = mid[...]
    gate = jax.nn.silu(dot_nt(act_in, gate_buf[...]))
    up_u[1].forward()
    dn_u[1].send()
    each(next_u[:3], "send")
    each(up_u, "arrive")
    act = (gate * dot_nt(act_in, up_buf[...])).astype(BF16)
    each(next_u[3:], "send")
    each(dn_u, "forward")
    each(dn_u, "arrive")
    part[1] = dot_nn(act, dn_buf[...])
    sum_d.scatter_start()
    each(next_u[:2], "forward")
    h_new = (h_mid + sum_d.total()).astype(BF16)
    h_out[...] = h_new
    sum_d.spread_start(norm_rows(h_new.astype(F32), gains[1:2, :]))
    each(next_u[2:], "forward")
    sum_d.spread_finish()
    each(next_u, "arrive")
    each(every, "finish")
    each(crossing, "finish")
    for copy in loads[1:]:
        copy.wait()


def last_layer_kernel(tg_size, sizes, attn, h_in, gains, o1, gate_held, up_held, dn_held, w_gu, w_dn,
                      hidden_out, gate_buf, up_buf, dn_buf, part, slots, mid, sum_send, sum_recv, *sems):
    place = Place(tg_size)
    make = Maker(place, sems, sizes)
    gate_u = make.gather("gate", 1, w_gu, gate_buf, HALVES, gate_held)
    up_u = make.gather("up", 1, w_gu, up_buf, HALVES, up_held)
    dn_u = make.gather("dn", 1, w_dn, dn_buf, HALVES, dn_held)
    every = gate_u + up_u + dn_u
    sum_o = SumOverTg(place, part.at[0], slots.at[0], mid, (sum_send.at[0], sum_recv.at[0]))
    sum_d = SumOverTg(place, part.at[1], slots.at[1], hidden_out, (sum_send.at[1], sum_recv.at[1]))

    place.barrier(True)
    each(every, "start")
    part[0] = dot_nn(attn[...], o1[...])
    sum_o.scatter_start()
    each(every, "send")
    each(gate_u, "forward")
    h_mid = (h_in[...].astype(F32) + sum_o.total()).astype(BF16).astype(F32)
    sum_o.spread_start(norm_rows(h_mid, gains[3:4, :]))
    each(up_u, "forward")
    sum_o.spread_finish()
    each(gate_u, "arrive")
    act_in = mid[...]
    gate = jax.nn.silu(dot_nt(act_in, gate_buf[...]))
    each(dn_u, "forward")
    each(up_u, "arrive")
    act = (gate * dot_nt(act_in, up_buf[...])).astype(BF16)
    each(dn_u, "arrive")
    part[1] = dot_nn(act, dn_buf[...])
    sum_d.scatter_start()
    h_new = (h_mid + sum_d.total()).astype(BF16)
    sum_d.spread_start(h_new)
    each(every, "finish")
    sum_d.spread_finish()


def store_kernel(layer, gate, up, prior, gen_gu, sem):
    ffn = gate.shape[0]
    copies = [pltpu.make_async_copy(src, gen_gu.at[layer, pl.ds(k * ffn, ffn)], sem.at[k])
              for k, src in enumerate([gate, up])]
    for copy in copies:
        copy.start()
    for copy in copies:
        copy.wait()


def remote_params(collective_id):
    return pltpu.CompilerParams(collective_id=collective_id, has_side_effects=True,
                                vmem_limit_bytes=32 * 1024 * 1024)


def solution(mesh):
    merge = mesh.shape["grp"]
    tg_size = mesh.shape["tg"]
    cache_spec = P(None, ROW_AXES, None, "tg", None)
    in_specs = (P(ROW_AXES, None), P(ROW_AXES), cache_spec, cache_spec,
                P("pp", None), P("pp", TRAIN_AXES, None), P("pp", None, TRAIN_AXES),
                P("pp", None), P("pp", TRAIN_AXES, None), P("pp", None, TRAIN_AXES))
    out_specs = (P(ROW_AXES, None), cache_spec, cache_spec, P(None, "tg", None), P(None, "tg", None))

    def body(hidden_in, seq_lens, k_cache, v_cache, attn_gain, w_qkv, w_o, mlp_gain, w_gate_up, w_down):
        batch, dim = hidden_in.shape
        layers, _, cache_len, kv_loc, head_dim = k_cache.shape
        width = kv_loc * head_dim
        ffn_rows = w_gate_up.shape[1] // 2
        ffn = ffn_rows * merge
        sizes = (head_dim, ffn_rows, merge)
        quarter = batch // tg_size
        w_qkv, w_gate_up = w_qkv[0], w_gate_up[0]
        w_o_t, w_down_t = jnp.transpose(w_o[0]), jnp.transpose(w_down[0])
        flat = lambda cache: jnp.transpose(cache, (0, 1, 3, 4, 2)).reshape(layers, batch, width, cache_len)
        k_flat, v_flat = flat(k_cache), flat(v_cache)
        dma = pltpu.SemaphoreType.DMA
        sds = jax.ShapeDtypeStruct
        layer_kv = sds((batch, width, cache_len), BF16)
        merged_qkv, merged_o, merged_ffn = (sds((3 * width, dim), BF16), sds((width, dim), BF16), sds((ffn, dim), BF16))
        act, held = sds((batch, dim), BF16), sds((ffn_rows, dim), BF16)
        rope = sds((head_dim // 2, batch), F32)
        sum_scratch = [pltpu.VMEM((2, batch, dim), F32), pltpu.VMEM((2, tg_size - 1, quarter, dim), F32),
                       pltpu.VMEM((batch, dim), BF16)]
        sum_sems = [dma((2, 2, tg_size - 1)), dma((2, 2, tg_size - 1))]

        normed, gains, cos_t, sin_t, qkv0, o0, k_now, v_now, gate_held = pl.pallas_call(
            functools.partial(first_kernel, tg_size, sizes, layers),
            in_specs=[HBM, VMEM] + [HBM] * 7, out_specs=[VMEM] * 8 + [HBM],
            out_shape=[act, sds((4, dim), F32), rope, rope, merged_qkv, merged_o, layer_kv, layer_kv, held],
            scratch_shapes=[pltpu.VMEM((batch, dim), BF16), pltpu.VMEM((2, 1, dim), BF16),
                            pltpu.VMEM((2, 1, dim), BF16), dma((5,)), dma((2,)), dma((2,))] + gather_sems(8),
            compiler_params=remote_params(1), name="first",
        )(hidden_in, seq_lens.reshape(1, batch), attn_gain, mlp_gain, w_qkv, w_o_t, w_gate_up, k_flat, v_flat)

        k_out, v_out, gen_qkv, attn = attend(0, seq_lens, normed, qkv0, cos_t, sin_t, k_now, v_now, head_dim, layers)

        normed, h_own, gate0, up0, qkv1, o1, k_now, v_now, up_held, dn_held = pl.pallas_call(
            functools.partial(first_layer_kernel, tg_size, sizes),
            in_specs=[VMEM, HBM, VMEM, VMEM] + [HBM] * 7,
            out_specs=[VMEM] * 8 + [HBM, HBM],
            out_shape=[act, sds((quarter, dim), BF16), merged_ffn, merged_ffn, merged_qkv, merged_o,
                       layer_kv, layer_kv, held, held],
            scratch_shapes=[pltpu.VMEM((ffn, dim), BF16)] + sum_scratch + [
                pltpu.VMEM((quarter, dim), BF16), dma((3,))] + sum_sems + gather_sems(14),
            compiler_params=remote_params(2), name="layer_0",
        )(attn, hidden_in, gains, o0, gate_held, w_qkv, w_o_t, w_gate_up, w_down_t, k_flat, v_flat)

        k_out, v_out, gen_qkv, gen_gate_up, attn = attend(
            1, seq_lens, normed, qkv1, cos_t, sin_t, k_now, v_now, head_dim, layers,
            (gate0, up0), (k_out, v_out, gen_qkv))

        hidden, gate1, up1 = pl.pallas_call(
            functools.partial(last_layer_kernel, tg_size, sizes),
            in_specs=[VMEM] * 4 + [HBM] * 5, out_specs=[VMEM] * 3,
            out_shape=[act, merged_ffn, merged_ffn],
            scratch_shapes=[pltpu.VMEM((ffn, dim), BF16)] + sum_scratch + sum_sems + gather_sems(6),
            compiler_params=remote_params(3), name="layer_1",
        )(attn, h_own, gains, o1, gate_held, up_held, dn_held, w_gate_up, w_down_t)

        gen_gate_up = pl.pallas_call(
            functools.partial(store_kernel, 1),
            in_specs=[VMEM, VMEM, HBM], out_specs=HBM, out_shape=sds(gen_gate_up.shape, BF16),
            scratch_shapes=[dma((2,))], input_output_aliases={2: 0}, name="store",
        )(gate1, up1, gen_gate_up)

        unflat = lambda cache: jnp.transpose(
            cache.reshape(layers, batch, kv_loc, head_dim, cache_len), (0, 1, 4, 2, 3))
        return hidden, unflat(k_out), unflat(v_out), gen_qkv, gen_gate_up

    return jax.shard_map(body, mesh=mesh, in_specs=in_specs, out_specs=out_specs, check_vma=False)
```

time: 158 us -> 158 us (level)
  the two profiles are of different devices: /device:TPU:0 before, /device:TPU:6 now
where the time goes in v2:
time: 158 us; the launch traced here: 157 us
  Pallas kernels  144 us (91%)
  local copies, waits for them, and re-layouts  12.2 us (8%)
    pallas_call x1, Pallas kernels, body(): pl.pallas_call(functools.partial(last_layer_kernel, tg_size, sizes), in_s...  54.3 us
    pallas_call x1, Pallas kernels, body(): pl.pallas_call(functools.partial(first_layer_kernel, tg_size, sizes), in_...  46.9 us
    pallas_call x1, Pallas kernels, body(): pl.pallas_call(functools.partial(first_kernel, tg_size, sizes, layers), i...  26.4 us
    pallas_call x2, Pallas kernels, attend(): pl.pallas_call(functools.partial(attend_kernel, layer, head_dim, len(prio...  13.4 us
    unnamed x33, local copies, waits for them, and re-layouts  12.2 us
    pallas_call x1, Pallas kernels, body(): pl.pallas_call(functools.partial(store_kernel, 1), in_specs=[VMEM, VMEM,...  3.39 us

profile of v2, /device:TPU:6, one launch (start us, length us, event | category | flops | bytes accessed | tf_op | source)
XLA Modules:
  0.0 157.4 jit_solution(63229140339650606)
XLA Ops:
  0.6 0.0 copy-start
  0.6 3.4 %copy-done = bf16[2,64,128,4,64]{2,4,3,1,0:T(8,128)(2,1)S(1)} copy-done((bf16[2,64,128,4,64]{2,4,3,1,0:T(8,128)(2,1)S(1)}, bf16[2,64,128,4,64]{2,4,3,1,0:T(8,128)(2,1)}, u32[]{:S(2)}) %copy-start) | copy-done | bytes 8388632
  4.0 0.0 copy-start.1
  4.0 1.1 copy-done.1
  5.1 0.0 copy-start.3
  5.1 1.0 copy-done.3
  6.1 0.0 copy-start.8
  6.1 0.9 copy-done.8
  7.0 0.0 copy-start.10
  7.0 0.9 copy-done.10
  7.9 0.0 copy-start.12
  7.9 0.7 copy-done.12
  8.6 0.0 copy-start.14
  8.6 0.7 copy-done.14
  9.3 0.0 copy-start.15
  9.3 0.7 copy-done.15
  10.0 26.4 %first.1 = (bf16[64,1024]{1,0:T(8,128)(2,1)S(1)}, f32[4,1024]{1,0:T(4,128)S(1)}, f32[32,64]{1,0:T(8,128)S(1)}, f32[32,64]{1,0:T(8,128)S(1)}, bf16[768,1024]{1,0:...) custom-call(bf16[64,1024]{1,0:T(8,128)(2,1)S(1)} %copy-done.8, ...), custom_call_target="tpu_custom_call" | custom-call | tf_op jit(solution)/shard_map/first/pallas_call | solution.py:597
  36.4 0.0 copy-start.2
  36.4 0.0 copy-start.4
  36.4 0.0 copy-start.7
  36.4 0.0 copy-start.9
  36.4 0.0 copy-start.11
  36.4 6.7 %attend_0.1 = (bf16[2,64,256,128]{3,2,1,0:T(8,128)(2,1)}, bf16[2,64,256,128]{3,2,1,0:T(8,128)(2,1)}, bf16[2,768,1024]{2,1,0:T(8,128)(2,1)}, bf16[64,256]{1,0:T(8,128)(2,1)S(1)}) custom-call(s32[64]{0:T(128)S(1)} %copy-done.12, bf16[64,1024]{1,0:T(8,128)(2,1)S(1)} %get-tuple-element.36.normed, bf16[768,1024]{1,0:T(8,128)(2,1)S(1)} %get-tuple-element.37.w_qkv, ...), custom_call_target="tpu_custom_call" | custom-call | tf_op jit(solution)/shard_map/attend_0/pallas_call | solution.py:438
  43.1 0.0 copy-done.2
  43.1 0.0 copy-done.4
  43.2 0.0 copy-done.7
  43.2 0.0 copy-done.9
  43.2 0.0 copy-done.11
  43.2 0.0 copy-start.13
  43.2 46.9 %layer_0.1 = (bf16[64,1024]{1,0:T(8,128)(2,1)S(1)}, bf16[16,1024]{1,0:T(8,128)(2,1)S(1)}, bf16[704,1024]{1,0:T(8,128)(2,1)S(1)}, bf16[704,1024]{1,0:T(8,128)(2,1...) custom-call(bf16[64,256]{1,0:T(8,128)(2,1)S(1)} %get-tuple-element.4, ...), custom_call_target="tpu_custom_call" | custom-call | tf_op jit(solution)/shard_map/layer_0/pallas_call | solution.py:608
  90.1 0.0 copy-done.13
  90.1 6.7 %attend_1.1 = (bf16[2,64,256,128]{3,2,1,0:T(8,128)(2,1)}, bf16[2,64,256,128]{3,2,1,0:T(8,128)(2,1)}, bf16[2,768,1024]{2,1,0:T(8,128)(2,1)}, bf16[2,1408,1024]{2,1,0:T(8,128)(2,1)}, bf16[64,256]{1,0:T(8,128)(2,1)S(1)}) custom-call(s32[64]{0:T(128)S(1)} %copy-done.13, ...), custom_call_target="tpu_custom_call", output_to_operand_aliasing={{0}: (9, {}), {1}: (10, {}), {2}: (11, {})} | custom-call | tf_op jit(solution)/shard_map/attend_1/pallas_call | solution.py:438
  96.8 54.3 %layer_1.1 = (bf16[64,1024]{1,0:T(8,128)(2,1)S(1)}, bf16[704,1024]{1,0:T(8,128)(2,1)S(1)}, bf16[704,1024]{1,0:T(8,128)(2,1)S(1)}) custom-call(bf16[64,256]{1,0:T(8,128)(2,1)S(1)} %get-tuple-element.55.attn, bf16[16,1024]{1,0:T(8,128)(2,1)S(1)} %get-tuple-element.56.h_in, f32[4,1024]{1,0:T(4,128)S(1)} %get-tuple-element.43.gains, ...), custom_call_target="tpu_custom_call" | custom-call | tf_op jit(solution)/shard_map/layer_1/pallas_call | solution.py:623
  151.1 0.0 copy-start.5
  151.2 1.1 copy-done.5
  152.3 0.0 copy-start.6
  152.3 1.1 copy-done.6
  153.4 3.4 %store.1 = bf16[2,1408,1024]{2,1,0:T(8,128)(2,1)} custom-call(bf16[704,1024]{1,0:T(8,128)(2,1)} %copy-done.5, bf16[704,1024]{1,0:T(8,128)(2,1)} %copy-done.6, bf16[2,1408,1024]{2,1,0:T(8,128)(2,1)} %get-tuple-element.66.prior), custom_call_target="tpu_custom_call", output_to_operand_aliasing={{}: (2, {})} | custom-call | tf_op jit(solution)/shard_map/store/pallas_call | solution.py:631
  156.8 0.7 copy.24
Async XLA Ops:
  0.6 3.4 %copy-start = (bf16[2,64,128,4,64]{2,4,3,1,0:T(8,128)(2,1)S(1)}, bf16[2,64,128,4,64]{2,4,3,1,0:T(8,128)(2,1)}, u32[]{:S(2)}) copy-start(bf16[2,64,128,4,64]{2,4,3,1,0:T(8,128)(2,1)} %param.12) | copy-start | bytes 25165828
  4.0 1.1 copy-start.1
  5.1 1.0 copy-start.3
  6.1 0.9 copy-start.8
  7.0 0.9 copy-start.10
  7.9 0.7 copy-start.12
  8.6 0.7 copy-start.14
  9.3 0.7 copy-start.15
  36.4 6.8 %copy-start.2 = (bf16[1,352,1024]{2,1,0:T(8,128)(2,1)S(1)}, bf16[1,352,1024]{2,1,0:T(8,128)(2,1)}, u32[]{:S(2)}) copy-start(bf16[1,352,1024]{2,1,0:T(8,128)(2,1)} %param.18) | copy-start | bytes 2162692
  36.4 6.8 %copy-start.4 = (bf16[1,192,1024]{2,1,0:T(8,128)(2,1)S(1)}, bf16[1,192,1024]{2,1,0:T(8,128)(2,1)}, u32[]{:S(2)}) copy-start(bf16[1,192,1024]{2,1,0:T(8,128)(2,1)} %param.15) | copy-start | bytes 1179652
  36.4 6.8 %copy-start.7 = (bf16[1,1024,176]{1,2,0:T(8,128)(2,1)S(1)}, bf16[1,1024,176]{1,2,0:T(8,128)(2,1)}, u32[]{:S(2)}) copy-start(bf16[1,1024,176]{1,2,0:T(8,128)(2,1)} %param.19) | copy-start | bytes 1081348
  36.4 6.8 %copy-start.9 = (bf16[64,1024]{1,0:T(8,128)(2,1)S(1)}, bf16[64,1024]{1,0:T(8,128)(2,1)}, u32[]{:S(2)}) copy-start(bf16[64,1024]{1,0:T(8,128)(2,1)} %hidden.3) | copy-start | bytes 393220
  36.4 6.8 %copy-start.11 = (bf16[1,1024,64]{1,2,0:T(8,128)(2,1)S(1)}, bf16[1,1024,64]{1,2,0:T(8,128)(2,1)}, u32[]{:S(2)}) copy-start(bf16[1,1024,64]{1,2,0:T(8,128)(2,1)} %param.16) | copy-start | bytes 393220
  43.2 46.9 %copy-start.13 = (s32[64]{0:T(128)S(1)}, s32[64]{0:T(128)}, u32[]{:S(2)}) copy-start(s32[64]{0:T(128)} %lens.3) | copy-start | bytes 772
  151.1 1.1 copy-start.5
  152.3 1.1 copy-start.6

commit v3 on v2

v3 whole, which is shorter than its diff:
```python
import functools
import math

import jax
import jax.numpy as jnp
from jax import lax
from jax.experimental import pallas as pl
from jax.experimental.pallas import tpu as pltpu
from jax.sharding import PartitionSpec as P

ROPE_THETA = 500000.0
NORM_EPS = 1e-5
MASK_FILL = -1e30
ROW_AXES = ("pp", "grp")
TRAIN_AXES = ("tg", "grp")
BF16 = jnp.bfloat16
F32 = jnp.float32
MESH = pl.DeviceIdType.MESH
HBM = pl.BlockSpec(memory_space=pltpu.HBM)
SMEM = pl.BlockSpec(memory_space=pltpu.SMEM)
VMEM = pl.BlockSpec(memory_space=pltpu.VMEM)
SEQ_TILE = 16
HEAD_ROWS = 8


def norm_rows(hidden_f32, gain_row):
    inv_rms = lax.rsqrt(jnp.mean(hidden_f32 * hidden_f32, axis=-1, keepdims=True) + NORM_EPS)
    return (hidden_f32 * inv_rms * gain_row).astype(BF16)


def rows(ref, start, count):
    return ref.at[pl.ds(pl.multiple_of(start, 16), count), :]


class Place:
    def __init__(self, tg_size):
        self.tg_size = tg_size
        self.tg = lax.axis_index("tg")
        self.pp = lax.axis_index("pp")
        self.grp = lax.axis_index("grp")
        self.partner = self.grp + 1 - 2 * lax.rem(self.grp, 2)
        self.across = lax.rem(self.grp + 2, 4)
        self.diagonal = lax.rem(self.partner + 2, 4)
        self.stage = 1 - self.pp

    def tg_at(self, step):
        return lax.rem(self.tg + step, self.tg_size)

    def barrier(self, with_tg):
        sem = pltpu.get_barrier_semaphore()
        targets = [{"grp": self.partner}, {"grp": self.across}, {"pp": self.stage}]
        if with_tg:
            targets += [{"tg": self.tg_at(step)} for step in range(1, self.tg_size)]
        for target in targets:
            pl.semaphore_signal(sem, inc=1, device_id=target, device_id_type=MESH)
        pl.semaphore_wait(sem, len(targets))


def gather_sems(count):
    dma = pltpu.SemaphoreType.DMA
    return [dma((count,)), dma((count, 2)), dma((count, 2)), dma((count, 2)), dma((count, 2, 2))]


class Cross:
    def __init__(self, place, sems, index, layer, own, held):
        self.place, self.layer = place, layer
        self.copy = lambda: pltpu.make_async_remote_copy(
            src_ref=own, dst_ref=held, send_sem=sems[1].at[index, 0], recv_sem=sems[1].at[index, 1],
            device_id={"pp": place.stage}, device_id_type=MESH)

    def start(self):
        @pl.when(self.place.pp == self.layer)
        def _():
            self.copy().start()

    def finish(self):
        @pl.when(self.place.pp == self.layer)
        def _():
            self.copy().wait_send()

        @pl.when(self.place.pp != self.layer)
        def _():
            self.copy().wait_recv()


class Gather:
    def __init__(self, place, sems, index, layer, own, held, buf, base, stride, count, route):
        self.place, self.layer, self.own, self.held, self.buf = place, layer, own, held, buf
        self.base, self.stride, self.count, self.route = base, stride, count, route
        local, ysem, zsem, xsem, psem = sems
        self.local = local.at[index]
        self.ysem = (ysem.at[index, 0], ysem.at[index, 1])
        self.zsem = (zsem.at[index, 0], zsem.at[index, 1])
        self.xsem = (xsem.at[index, 0], xsem.at[index, 1])
        self.psem = [(psem.at[index, k, 0], psem.at[index, k, 1]) for k in range(2)]

    def on(self, owner, body):
        pl.when(self.place.pp == self.layer if owner else self.place.pp != self.layer)(body)

    def at(self, grp):
        return rows(self.buf, self.base + grp * self.stride, self.count)

    def remote(self, src, grp, sems, target):
        return pltpu.make_async_remote_copy(
            src_ref=src, dst_ref=self.at(grp), send_sem=sems[0], recv_sem=sems[1],
            device_id=target, device_id_type=MESH)

    def local_copy(self, src):
        return pltpu.make_async_copy(src, self.at(self.place.grp), self.local)

    def y_copy(self):
        return self.remote(self.own, self.place.grp, self.ysem, {"pp": self.place.stage})

    def z_copy(self):
        grp = self.place.across
        return self.remote(self.at(grp), grp, self.zsem, {"pp": self.place.stage})

    def x_copy(self, grp):
        return self.remote(self.at(grp), grp, self.xsem, {"grp": self.place.across})

    def p_copy(self, grp, which):
        return self.remote(self.at(grp), grp, self.psem[which], {"grp": self.place.partner})

    def start(self):
        def owner():
            if self.held is None:
                self.y_copy().start()
            self.local_copy(self.own).start()

        self.on(True, owner)
        if self.held is not None:
            self.on(False, lambda: self.local_copy(self.held).start())

    def send(self):
        self.on(True, lambda: self.local_copy(self.own).wait())
        if self.held is None:
            self.on(False, lambda: self.y_copy().wait_recv())
        else:
            self.on(False, lambda: self.local_copy(self.held).wait())
        grp = self.place.grp
        if self.route == "both":
            self.x_copy(grp).start()
        else:
            self.on(self.route == "owner", lambda: self.x_copy(grp).start())
        self.p_copy(grp, 0).start()

    def relay(self):
        grp = self.place.across

        def pass_on():
            self.x_copy(grp).wait_recv()
            if self.route != "both":
                self.z_copy().start()
            self.p_copy(grp, 1).start()

        if self.route == "both":
            pass_on()
        else:
            self.on(self.route == "owner", pass_on)

    def receive(self):
        def take():
            self.z_copy().wait_recv()
            self.p_copy(self.place.across, 1).start()

        if self.route != "both":
            self.on(self.route != "owner", take)

    def arrive(self):
        self.p_copy(self.place.partner, 0).wait_recv()
        self.p_copy(self.place.diagonal, 1).wait_recv()

    def finish(self):
        if self.held is None:
            self.on(True, lambda: self.y_copy().wait_send())
        grp = self.place.grp
        if self.route == "both":
            self.x_copy(grp).wait_send()
        else:
            def relayed():
                self.x_copy(grp).wait_send()
                self.z_copy().wait_send()

            self.on(self.route == "owner", relayed)
        self.p_copy(grp, 0).wait_send()
        self.p_copy(self.place.across, 1).wait_send()


class Maker:
    def __init__(self, place, sems, sizes):
        self.place, self.sems, self.sizes, self.index = place, sems, sizes, 0

    def gather(self, kind, layer, src_ref, buf, routes, held=None):
        out = []
        for k, (src, hold, base, stride, count) in enumerate(row_blocks(kind, self.sizes)):
            route = routes[k % len(routes)]
            out.append(Gather(self.place, self.sems, self.index, layer, src_ref.at[pl.ds(src, count), :],
                              None if held is None else held.at[pl.ds(hold, count), :],
                              buf, base, stride, count, route))
            self.index += 1
        return out

    def cross(self, kind, layer, src_ref, held):
        count = self.sizes[1]
        src = count if kind == "up" else 0
        piece = Cross(self.place, self.sems, self.index, layer, src_ref.at[pl.ds(src, count), :], held)
        self.index += 1
        return [piece]


def each(units, what):
    for unit in units:
        getattr(unit, what)()


class Flow:
    def __init__(self, units, lag):
        self.events, self.done = [], 0
        for k in range(len(units) + lag):
            if k < len(units):
                self.events.append((units[k], "send"))
            if k >= lag:
                self.events.append((units[k - lag], "relay"))

    def through(self, unit, what):
        last = self.events.index((unit, what))
        while self.done <= last:
            piece, step = self.events[self.done]
            getattr(piece, step)()
            self.done += 1


def row_pieces(count, parts):
    size = (-(-count // parts) + 15) // 16 * 16
    return [(off, min(size, count - off)) for off in range(0, count, size)]


def row_blocks(kind, sizes):
    head_rows, ffn_rows, merge = sizes
    if kind in ("qkv", "o"):
        return [(k * head_rows + off, k * head_rows + off, k * merge * head_rows + off, head_rows, count)
                for k in range(3 if kind == "qkv" else 1) for off, count in row_pieces(head_rows, 2)]
    shift = ffn_rows if kind == "up" else 0
    return [(shift + off, off, off, ffn_rows, count) for off, count in row_pieces(ffn_rows, 4)]


class SumOverTg:
    def __init__(self, place, part, slots, full, sems):
        self.place, self.part, self.slots, self.full = place, part, slots, full
        self.count = slots.shape[1]
        self.send, self.recv = sems

    def scatter_copy(self, step):
        peer = self.place.tg_at(step)
        return pltpu.make_async_remote_copy(
            src_ref=rows(self.part, peer * self.count, self.count), dst_ref=self.slots.at[step - 1],
            send_sem=self.send.at[0, step - 1], recv_sem=self.recv.at[0, step - 1],
            device_id={"tg": peer}, device_id_type=MESH)

    def spread_copy(self, step):
        own = rows(self.full, self.place.tg * self.count, self.count)
        return pltpu.make_async_remote_copy(
            src_ref=own, dst_ref=own,
            send_sem=self.send.at[1, step - 1], recv_sem=self.recv.at[1, step - 1],
            device_id={"tg": self.place.tg_at(step)}, device_id_type=MESH)

    def spread_wait(self, step):
        peer = self.place.tg_at(self.place.tg_size - step)
        block = rows(self.full, peer * self.count, self.count)
        pltpu.make_async_remote_copy(
            src_ref=block, dst_ref=block,
            send_sem=self.send.at[1, step - 1], recv_sem=self.recv.at[1, step - 1],
            device_id={"tg": peer}, device_id_type=MESH).wait_recv()

    def steps(self):
        return range(1, self.place.tg_size)

    def far_first(self):
        return self.steps()

    def scatter_start(self):
        for step in self.far_first():
            self.scatter_copy(step).start()

    def total(self):
        for step in self.steps():
            self.scatter_copy(step).wait_recv()
        out = self.part[pl.ds(pl.multiple_of(self.place.tg * self.count, self.count), self.count), :]
        for step in self.steps():
            out = out + self.slots[step - 1]
        return out

    def spread_start(self, block):
        self.full[pl.ds(pl.multiple_of(self.place.tg * self.count, self.count), self.count), :] = block
        for step in self.steps():
            self.scatter_copy(step).wait_send()
        for step in self.far_first():
            self.spread_copy(step).start()

    def spread_finish(self):
        for step in self.steps():
            self.spread_wait(step)
        for step in self.steps():
            self.spread_copy(step).wait_send()


def dot_nt(lhs, rhs):
    return lax.dot_general(lhs, rhs, (((1,), (1,)), ((), ())), preferred_element_type=F32)


def dot_nn(lhs, rhs):
    return jnp.dot(lhs, rhs, preferred_element_type=F32)


BOTH, HALVES = ("both",), ("owner", "other")


def project(w_qkv, normed, cos_v, sin_v, head_dim, q_scr, k_scr, v_scr):
    batch, width = q_scr.shape
    half = head_dim // 2
    proj = dot_nt(w_qkv, normed)

    def rope(block):
        pieces = []
        for row in range(0, width, head_dim):
            first, second = block[row:row + half], block[row + half:row + head_dim]
            pieces += [first * cos_v - second * sin_v, second * cos_v + first * sin_v]
        return jnp.concatenate(pieces, axis=0).astype(BF16).astype(F32)

    q_scr[...] = jnp.transpose(rope(proj[:width])) * (head_dim ** -0.5)
    pad = jnp.zeros((width, k_scr.shape[1] - batch), F32)
    k_scr[...] = jnp.concatenate([rope(proj[width:2 * width]), pad], axis=1)
    v_scr[...] = jnp.concatenate([proj[2 * width:].astype(BF16).astype(F32), pad], axis=1)


def attend_tile(seq0, head_dim, lens, place_k, place_v, q_scr, k_in, v_in, k_new, v_new, after_keys):
    width, cache_len = k_in.shape[1:]
    own_head = (lax.broadcasted_iota(jnp.int32, (HEAD_ROWS, width), 1) // head_dim
                == lax.broadcasted_iota(jnp.int32, (HEAD_ROWS, width), 0))
    lane_row = lax.broadcasted_iota(jnp.int32, (HEAD_ROWS, cache_len), 1)
    scores = []
    for j in range(SEQ_TILE):
        length = lens[seq0 + j]
        k_val = place_k(length, j, k_in[seq0 + j])
        k_new[seq0 + j] = k_val
        q_block = jnp.where(own_head, q_scr[pl.ds(seq0 + j, 1), :], 0.0).astype(BF16)
        scores.append(jnp.where(lane_row <= length, dot_nn(q_block, k_val), MASK_FILL))
    after_keys()
    score = jnp.concatenate(scores, axis=0)
    expo = jnp.exp(score - jnp.max(score, axis=-1, keepdims=True))
    probs = (expo / jnp.sum(expo, axis=-1, keepdims=True)).astype(BF16)
    outs = []
    for j in range(SEQ_TILE):
        v_val = place_v(lens[seq0 + j], j, v_in[seq0 + j])
        v_new[seq0 + j] = v_val
        mixed = dot_nt(probs[j * HEAD_ROWS:(j + 1) * HEAD_ROWS], v_val)
        outs.append(jnp.sum(jnp.where(own_head, mixed, 0.0), axis=0, keepdims=True))
    return jnp.concatenate(outs, axis=0).astype(BF16)


def opening_kernel(tg_size, sizes, lens, lens_row, hidden, attn_gain, mlp_gain, w_qkv, w_o, w_gu, w_dn, k_cache, v_cache,
                   normed, h_out, gains, cos_t, sin_t, gate_buf, up_buf, qkv0, qkv1, o1, k_first, v_first,
                   k_next, v_next, gate_held, up_held, dn_held,
                   o_buf, dn_buf, part, slots, mid, hidden_buf, first_norm, attn, q_scr, k_scr, v_scr, own_gain, far_gain,
                   load_sem, gain_send, gain_recv, sum_send, sum_recv, *sems):
    head_dim = sizes[0]
    place = Place(tg_size)
    make = Maker(place, sems, sizes)
    qkv_u = make.gather("qkv", 0, w_qkv, qkv0, BOTH)
    o_u = make.gather("o", 0, w_o, o_buf, BOTH)
    gate_u = make.gather("gate", 0, w_gu, gate_buf, BOTH)
    up_u = make.gather("up", 0, w_gu, up_buf, BOTH)
    dn_u = make.gather("dn", 0, w_dn, dn_buf, BOTH)
    now_u = qkv_u + o_u + gate_u + up_u + dn_u
    next_u = make.gather("qkv", 1, w_qkv, qkv1, BOTH) + make.gather("o", 1, w_o, o1, BOTH)
    crossing = (make.cross("gate", 1, w_gu, gate_held) + make.cross("up", 1, w_gu, up_held)
                + make.cross("dn", 1, w_dn, dn_held))
    flow = Flow(now_u, 2)
    sum_o = SumOverTg(place, part.at[0], slots.at[0], mid, (sum_send.at[0], sum_recv.at[0]))
    sum_d = SumOverTg(place, part.at[1], slots.at[1], normed, (sum_send.at[1], sum_recv.at[1]))
    count = slots.shape[2]
    loads = [pltpu.make_async_copy(src, dst, load_sem.at[k]) for k, (src, dst) in enumerate([
        (hidden, hidden_buf), (attn_gain, own_gain.at[0]), (mlp_gain, own_gain.at[1]),
        (k_cache.at[0], k_first), (v_cache.at[0], v_first), (k_cache.at[1], k_next), (v_cache.at[1], v_next)])]

    for copy in loads[:3]:
        copy.start()
    place.barrier(True)
    each(qkv_u + o_u, "start")
    for copy in loads[1:3]:
        copy.wait()
    gain_copies = [
        pltpu.make_async_remote_copy(
            src_ref=own_gain.at[k], dst_ref=far_gain.at[k], send_sem=gain_send.at[k], recv_sem=gain_recv.at[k],
            device_id={"pp": place.stage}, device_id_type=MESH) for k in range(2)]
    for copy in gain_copies:
        copy.start()
    each(gate_u + up_u + dn_u + next_u, "start")
    each(crossing, "start")
    for copy in loads[3:5]:
        copy.start()
    half = cos_t.shape[0]
    power = lax.broadcasted_iota(jnp.int32, cos_t.shape, 0).astype(F32) * (-math.log(ROPE_THETA) / half)
    angle = jnp.exp(power) * lens_row[...].astype(F32)
    cos_t[...] = jnp.cos(angle)
    sin_t[...] = jnp.sin(angle)
    flow.through(qkv_u[1], "send")
    loads[0].wait()
    for copy in gain_copies:
        copy.wait()
    first = place.pp == 0
    table = []
    for k in range(2):
        own_row, far_row = own_gain[k].astype(F32), far_gain[k].astype(F32)
        table.append(jnp.where(first, own_row, far_row))
        table.append(jnp.where(first, far_row, own_row))
    for k, row in enumerate(table):
        gains[pl.ds(k, 1), :] = row
    first_norm[...] = norm_rows(hidden_buf[...].astype(F32), table[0])
    flow.through(qkv_u[-1], "relay")
    each(qkv_u, "arrive")
    project(qkv0[...], first_norm[...], cos_t[...], sin_t[...], head_dim, q_scr, k_scr, v_scr)
    for copy in loads[3:5]:
        copy.wait()

    lane = lax.broadcasted_iota(jnp.int32, k_first.shape[1:], 1)
    marks = [(o_u[-1], "relay"), (gate_u[0], "relay"), (gate_u[1], "relay"), (gate_u[3], "send")]
    for tile, mark in enumerate(marks):
        seq0 = tile * SEQ_TILE
        k_cols, v_cols = k_scr[...].astype(BF16), v_scr[...].astype(BF16)
        put_k = lambda length, j, old: jnp.where(lane == length, k_cols[:, seq0 + j:seq0 + j + 1], old)
        put_v = lambda length, j, old: jnp.where(lane == length, v_cols[:, seq0 + j:seq0 + j + 1], old)
        attn[pl.ds(seq0, SEQ_TILE), :] = attend_tile(
            seq0, head_dim, lens, put_k, put_v, q_scr, k_first, v_first, k_first, v_first, lambda: None)
        flow.through(*mark)

    for copy in loads[5:]:
        copy.start()
    each(o_u, "arrive")
    part[0] = dot_nn(attn[...], o_buf[...])
    sum_o.scatter_start()
    flow.through(up_u[1], "relay")
    own_rows = hidden_buf[pl.ds(pl.multiple_of(place.tg * count, count), count), :]
    h_mid = (own_rows.astype(F32) + sum_o.total()).astype(BF16).astype(F32)
    sum_o.spread_start(norm_rows(h_mid, gains[2:3, :]))
    flow.through(up_u[-1], "relay")
    each(gate_u, "arrive")
    sum_o.spread_finish()
    act_in = mid[...]
    gate = jax.nn.silu(dot_nt(act_in, gate_buf[...]))
    each(up_u, "arrive")
    act = (gate * dot_nt(act_in, up_buf[...])).astype(BF16)
    flow.through(dn_u[-1], "send")
    each(next_u, "send")
    flow.through(dn_u[-1], "relay")
    each(dn_u, "arrive")
    part[1] = dot_nn(act, dn_buf[...])
    sum_d.scatter_start()
    each(next_u[:4], "relay")
    h_new = (h_mid + sum_d.total()).astype(BF16)
    h_out[...] = h_new
    sum_d.spread_start(norm_rows(h_new.astype(F32), gains[1:2, :]))
    each(next_u[4:], "relay")
    each(now_u, "finish")
    each(crossing, "finish")
    sum_d.spread_finish()
    each(next_u, "arrive")
    each(next_u, "finish")
    for copy in loads[5:]:
        copy.wait()


def attend_kernel(head_dim, lens, normed, w_qkv, cos_t, sin_t, k_in, v_in, w_first, gate, up, k_first, v_first,
                  k_out, v_out, gen_qkv, gen_gu, attn_out, k_new, v_new, q_scr, k_scr, v_scr, kv_sem, gen_sem):
    ffn = gate.shape[0]
    gens = [pltpu.make_async_copy(src, dst, gen_sem.at[k]) for k, (src, dst) in enumerate([
        (k_first, k_out.at[0]), (v_first, v_out.at[0]), (w_first, gen_qkv.at[0]), (w_qkv, gen_qkv.at[1]),
        (gate, gen_gu.at[0, pl.ds(0, ffn)]), (up, gen_gu.at[0, pl.ds(ffn, ffn)])])]
    for copy in gens:
        copy.start()
    batch, width = q_scr.shape
    cache_len = k_in.shape[2]
    project(w_qkv[...], normed[...], cos_t[...], sin_t[...], head_dim, q_scr, k_scr, v_scr)
    lane = lax.broadcasted_iota(jnp.int32, (width, cache_len), 1)

    def copy_out(k, i):
        block = pl.ds(i * SEQ_TILE, SEQ_TILE)
        new, out = [(k_new, k_out), (v_new, v_out)][k]
        return pltpu.make_async_copy(new.at[block], out.at[1, block], kv_sem.at[k, i])

    def step(i, carry):
        seq0 = i * SEQ_TILE

        def placer(cols):
            def place(length, j, old):
                moved = pltpu.roll(cols, lax.rem(length - seq0 - j + cache_len, cache_len), 1).astype(BF16)
                return jnp.where(lane == length, moved, old)

            return place

        out = attend_tile(seq0, head_dim, lens, placer(k_scr[...]), placer(v_scr[...]), q_scr, k_in, v_in, k_new, v_new,
                          lambda: copy_out(0, i).start())
        copy_out(1, i).start()
        attn_out[pl.ds(pl.multiple_of(seq0, SEQ_TILE), SEQ_TILE), :] = out
        return carry

    steps = batch // SEQ_TILE
    lax.fori_loop(0, steps, step, 0)
    for i in range(steps):
        copy_out(0, i).wait()
        copy_out(1, i).wait()
    for copy in gens:
        copy.wait()


def last_layer_kernel(tg_size, sizes, attn, h_in, gains, o1, gate_held, up_held, dn_held, w_gu, w_dn,
                      hidden_out, gate_buf, up_buf, dn_buf, part, slots, mid, sum_send, sum_recv, *sems):
    place = Place(tg_size)
    make = Maker(place, sems, sizes)
    gate_u = make.gather("gate", 1, w_gu, gate_buf, HALVES, gate_held)
    up_u = make.gather("up", 1, w_gu, up_buf, HALVES, up_held)
    dn_u = make.gather("dn", 1, w_dn, dn_buf, HALVES, dn_held)
    every = gate_u + up_u + dn_u
    sum_o = SumOverTg(place, part.at[0], slots.at[0], mid, (sum_send.at[0], sum_recv.at[0]))
    sum_d = SumOverTg(place, part.at[1], slots.at[1], hidden_out, (sum_send.at[1], sum_recv.at[1]))

    place.barrier(True)
    each(every, "start")
    part[0] = dot_nn(attn[...], o1[...])
    sum_o.scatter_start()
    each(every, "send")
    each(gate_u, "relay")
    h_mid = (h_in[...].astype(F32) + sum_o.total()).astype(BF16).astype(F32)
    sum_o.spread_start(norm_rows(h_mid, gains[3:4, :]))
    each(gate_u, "receive")
    each(up_u, "relay")
    each(gate_u, "arrive")
    sum_o.spread_finish()
    act_in = mid[...]
    gate = jax.nn.silu(dot_nt(act_in, gate_buf[...]))
    each(dn_u, "relay")
    each(up_u, "receive")
    each(up_u, "arrive")
    act = (gate * dot_nt(act_in, up_buf[...])).astype(BF16)
    each(dn_u, "receive")
    each(dn_u, "arrive")
    part[1] = dot_nn(act, dn_buf[...])
    sum_d.scatter_start()
    each(every, "finish")
    h_new = (h_mid + sum_d.total()).astype(BF16)
    sum_d.spread_start(h_new)
    sum_d.spread_finish()


def store_kernel(layer, gate, up, prior, gen_gu, sem):
    ffn = gate.shape[0]
    copies = [pltpu.make_async_copy(src, gen_gu.at[layer, pl.ds(k * ffn, ffn)], sem.at[k])
              for k, src in enumerate([gate, up])]
    for copy in copies:
        copy.start()
    for copy in copies:
        copy.wait()


MIB = 1024 * 1024
OPENING_VMEM, ATTEND_VMEM, LAST_VMEM = 34 * MIB, 34 * MIB, 34 * MIB


def remote_params(collective_id, limit):
    return pltpu.CompilerParams(collective_id=collective_id, has_side_effects=True, vmem_limit_bytes=limit)


def solution(mesh):
    merge = mesh.shape["grp"]
    tg_size = mesh.shape["tg"]
    cache_spec = P(None, ROW_AXES, None, "tg", None)
    in_specs = (P(ROW_AXES, None), P(ROW_AXES), cache_spec, cache_spec,
                P("pp", None), P("pp", TRAIN_AXES, None), P("pp", None, TRAIN_AXES),
                P("pp", None), P("pp", TRAIN_AXES, None), P("pp", None, TRAIN_AXES))
    out_specs = (P(ROW_AXES, None), cache_spec, cache_spec, P(None, "tg", None), P(None, "tg", None))

    def body(hidden_in, seq_lens, k_cache, v_cache, attn_gain, w_qkv, w_o, mlp_gain, w_gate_up, w_down):
        batch, dim = hidden_in.shape
        layers, _, cache_len, kv_loc, head_dim = k_cache.shape
        width = kv_loc * head_dim
        ffn_rows = w_gate_up.shape[1] // 2
        ffn = ffn_rows * merge
        sizes = (head_dim, ffn_rows, merge)
        quarter = batch // tg_size
        w_qkv, w_gate_up = w_qkv[0], w_gate_up[0]
        w_o_t, w_down_t = jnp.transpose(w_o[0]), jnp.transpose(w_down[0])
        flat = lambda cache: jnp.transpose(cache, (0, 1, 3, 4, 2)).reshape(layers, batch, width, cache_len)
        k_flat, v_flat = flat(k_cache), flat(v_cache)
        dma = pltpu.SemaphoreType.DMA
        sds = jax.ShapeDtypeStruct
        layer_kv = sds((batch, width, cache_len), BF16)
        merged_qkv, merged_o, merged_ffn = (sds((3 * width, dim), BF16), sds((width, dim), BF16), sds((ffn, dim), BF16))
        act, held = sds((batch, dim), BF16), sds((ffn_rows, dim), BF16)
        rope = sds((head_dim // 2, batch), F32)
        sum_scratch = [pltpu.VMEM((2, batch, dim), F32), pltpu.VMEM((2, tg_size - 1, quarter, dim), F32),
                       pltpu.VMEM((batch, dim), BF16)]
        sum_sems = [dma((2, 2, tg_size - 1)), dma((2, 2, tg_size - 1))]

        projected = [pltpu.VMEM((batch, width), F32), pltpu.VMEM((width, cache_len), F32),
                     pltpu.VMEM((width, cache_len), F32)]
        on_chip = lambda like: pltpu.VMEM(like.shape, like.dtype)
        off_chip = lambda like: pltpu.HBM(like.shape, like.dtype)
        hbm = lambda *arrays: [pltpu.with_memory_space_constraint(arr, pltpu.HBM) for arr in arrays]
        vmem = lambda *arrays: [pltpu.with_memory_space_constraint(arr, pltpu.VMEM) for arr in arrays]
        shared = [act, sds((quarter, dim), BF16), sds((4, dim), F32), rope, rope, merged_ffn, merged_ffn,
                  merged_qkv, merged_qkv, merged_o, layer_kv, layer_kv, layer_kv, layer_kv]
        (normed, h_own, gains, cos_t, sin_t, gate0, up0, qkv0, qkv1, o1, k_first, v_first, k_next, v_next,
         gate_held, up_held, dn_held) = pl.pallas_call(
            functools.partial(opening_kernel, tg_size, sizes),
            in_specs=[SMEM, VMEM] + [HBM] * 9, out_specs=[VMEM] * 14 + [HBM] * 3,
            out_shape=[on_chip(x) for x in shared] + [off_chip(held)] * 3,
            scratch_shapes=[pltpu.VMEM((width, dim), BF16), pltpu.VMEM((ffn, dim), BF16)] + sum_scratch + [
                pltpu.VMEM((batch, dim), BF16), pltpu.VMEM((batch, dim), BF16), pltpu.VMEM((batch, width), BF16)]
            + projected + [pltpu.VMEM((2, 1, dim), BF16), pltpu.VMEM((2, 1, dim), BF16),
                           dma((7,)), dma((2,)), dma((2,))] + sum_sems + gather_sems(31),
            compiler_params=remote_params(1, OPENING_VMEM), name="opening",
        )(seq_lens, seq_lens.reshape(1, batch), *hbm(hidden_in, attn_gain, mlp_gain, w_qkv, w_o_t, w_gate_up, w_down_t,
                                                     k_flat, v_flat))

        cache_shape = off_chip(k_flat)
        k_out, v_out, gen_qkv, gen_gate_up, attn = pl.pallas_call(
            functools.partial(attend_kernel, head_dim),
            in_specs=[SMEM] + [VMEM] * 11, out_specs=[HBM] * 4 + [VMEM],
            out_shape=[cache_shape, cache_shape, pltpu.HBM((layers, 3 * width, dim), BF16),
                       pltpu.HBM((layers, 2 * ffn, dim), BF16), pltpu.VMEM((batch, width), BF16)],
            scratch_shapes=[pltpu.VMEM(layer_kv.shape, BF16)] * 2 + projected + [
                dma((2, batch // SEQ_TILE)), dma((6,))],
            compiler_params=pltpu.CompilerParams(vmem_limit_bytes=ATTEND_VMEM), name="attend",
        )(seq_lens, *vmem(normed, qkv1, cos_t, sin_t, k_next, v_next, qkv0, gate0, up0, k_first, v_first))

        hidden, gate1, up1 = pl.pallas_call(
            functools.partial(last_layer_kernel, tg_size, sizes),
            in_specs=[VMEM] * 4 + [HBM] * 5, out_specs=[VMEM] * 3,
            out_shape=[on_chip(act), on_chip(merged_ffn), on_chip(merged_ffn)],
            scratch_shapes=[pltpu.VMEM((ffn, dim), BF16)] + sum_scratch + sum_sems + gather_sems(12),
            compiler_params=remote_params(2, LAST_VMEM), name="layer_1",
        )(*vmem(attn, h_own, gains, o1), *hbm(gate_held, up_held, dn_held, w_gate_up, w_down_t))

        gen_gate_up = pl.pallas_call(
            functools.partial(store_kernel, 1),
            in_specs=[VMEM, VMEM, HBM], out_specs=HBM, out_shape=pltpu.HBM(gen_gate_up.shape, BF16),
            scratch_shapes=[dma((2,))], input_output_aliases={2: 0}, name="store",
        )(*vmem(gate1, up1), gen_gate_up)

        unflat = lambda cache: jnp.transpose(
            cache.reshape(layers, batch, kv_loc, head_dim, cache_len), (0, 1, 4, 2, 3))
        return hidden, unflat(k_out), unflat(v_out), gen_qkv, gen_gate_up

    return jax.shard_map(body, mesh=mesh, in_specs=in_specs, out_specs=out_specs, check_vma=False)
```

time: 158 us -> 119 us (0.75)
  the two profiles are of different devices: /device:TPU:6 before, /device:TPU:0 now
where the time goes in v3:
time: 119 us
  Pallas kernels  118 us (99%)
    pallas_call x1, Pallas kernels, body(): pl.pallas_call(functools.partial(opening_kernel, tg_size, sizes), in_spec...  71.6 us
    pallas_call x1, Pallas kernels, body(): pl.pallas_call(functools.partial(last_layer_kernel, tg_size, sizes), in_s...  36.3 us
    pallas_call x1, Pallas kernels, body(): pl.pallas_call(functools.partial(attend_kernel, head_dim), in_specs=[SMEM...  8.44 us

profile of v3, /device:TPU:0, one launch (start us, length us, event | category | flops | bytes accessed | tf_op | source)
XLA Modules:
  0.0 119.2 jit_solution(7877674680536224765)
XLA Ops:
  0.6 71.6 %opening.1 = (bf16[64,1024]{1,0:T(8,128)(2,1)S(1)}, bf16[16,1024]{1,0:T(8,128)(2,1)S(1)}, f32[4,1024]{1,0:T(4,128)S(1)}, f32[32,64]{1,0:T(8,128)S(1)}, f32[32,64...) custom-call(s32[64]{0:T(128)} %lens.3, ...), custom_call_target="tpu_custom_call" | custom-call | tf_op jit(solution)/shard_map/opening/pallas_call | solution.py:613
  72.2 8.4 %attend.1 = (bf16[2,64,256,128]{3,2,1,0:T(8,128)(2,1)}, bf16[2,64,256,128]{3,2,1,0:T(8,128)(2,1)}, bf16[2,768,1024]{2,1,0:T(8,128)(2,1)}, bf16[2,1408,1024]{2,1,0:T(8,128)(2,1)}, bf16[64,256]{1,0:T(8,128)(2,1)S(1)}) custom-call(s32[64]{0:T(128)} %lens.3, bf16[64,1024]{1,0:T(8,128)(2,1)S(1)} %get-tuple-element.30.normed, ...), custom_call_target="tpu_custom_call" | custom-call | tf_op jit(solution)/shard_map/attend/pallas_call | solution.py:626
  80.7 36.3 %layer_1.1 = (bf16[64,1024]{1,0:T(8,128)(2,1)S(1)}, bf16[704,1024]{1,0:T(8,128)(2,1)S(1)}, bf16[704,1024]{1,0:T(8,128)(2,1)S(1)}) custom-call(bf16[64,256]{1,0:T(8,128)(2,1)S(1)} %get-tuple-element.41.attn, bf16[16,1024]{1,0:T(8,128)(2,1)S(1)} %get-tuple-element.42.h_in, f32[4,1024]{1,0:T(4,128)S(1)} %get-tuple-element.43.gains, ...), custom_call_target="tpu_custom_call" | custom-call | tf_op jit(solution)/shard_map/layer_1/pallas_call | solution.py:636
  117.0 0.7 copy.18
  117.6 1.6 %store.1 = bf16[2,1408,1024]{2,1,0:T(8,128)(2,1)} custom-call(bf16[704,1024]{1,0:T(8,128)(2,1)S(1)} %get-tuple-element.52.gate, bf16[704,1024]{1,0:T(8,128)(2,1)S(1)} %get-tuple-element.53.up, bf16[2,1408,1024]{2,1,0:T(8,128)(2,1)} %get-tuple-element.54.prior), custom_call_target="tpu_custom_call", output_to_operand_aliasing={{}: (2, {})} | custom-call | tf_op jit(solution)/shard_map/store/pallas_call | solution.py:644

commit v4 on v3

--- a/solution.py
+++ b/solution.py
@@ -359,8 +359,8 @@
 
 
 def opening_kernel(tg_size, sizes, lens, lens_row, hidden, attn_gain, mlp_gain, w_qkv, w_o, w_gu, w_dn, k_cache, v_cache,
-                   normed, h_out, gains, cos_t, sin_t, gate_buf, up_buf, qkv0, qkv1, o1, k_first, v_first,
-                   k_next, v_next, gate_held, up_held, dn_held,
+                   normed, h_out, gains, cos_t, sin_t, gate_buf, up_buf, gate1, qkv0, qkv1, o1, k_first, v_first,
+                   k_next, v_next, up_held, dn_held,
                    o_buf, dn_buf, part, slots, mid, hidden_buf, first_norm, attn, q_scr, k_scr, v_scr, own_gain, far_gain,
                    load_sem, gain_send, gain_recv, sum_send, sum_recv, *sems):
     head_dim = sizes[0]
@@ -372,9 +372,10 @@
     up_u = make.gather("up", 0, w_gu, up_buf, BOTH)
     dn_u = make.gather("dn", 0, w_dn, dn_buf, BOTH)
     now_u = qkv_u + o_u + gate_u + up_u + dn_u
-    next_u = make.gather("qkv", 1, w_qkv, qkv1, BOTH) + make.gather("o", 1, w_o, o1, BOTH)
-    crossing = (make.cross("gate", 1, w_gu, gate_held) + make.cross("up", 1, w_gu, up_held)
-                + make.cross("dn", 1, w_dn, dn_held))
+    next_u = make.gather("qkv", 1, w_qkv, qkv1, HALVES) + make.gather("o", 1, w_o, o1, HALVES)
+    late = len(next_u)
+    next_u += make.gather("gate", 1, w_gu, gate1, ("other", "owner"))
+    crossing = make.cross("up", 1, w_gu, up_held) + make.cross("dn", 1, w_dn, dn_held)
     flow = Flow(now_u, 2)
     sum_o = SumOverTg(place, part.at[0], slots.at[0], mid, (sum_send.at[0], sum_recv.at[0]))
     sum_d = SumOverTg(place, part.at[1], slots.at[1], normed, (sum_send.at[1], sum_recv.at[1]))
@@ -386,15 +387,13 @@
     for copy in loads[:3]:
         copy.start()
     place.barrier(True)
-    each(qkv_u + o_u, "start")
-    for copy in loads[1:3]:
-        copy.wait()
     gain_copies = [
         pltpu.make_async_remote_copy(
-            src_ref=own_gain.at[k], dst_ref=far_gain.at[k], send_sem=gain_send.at[k], recv_sem=gain_recv.at[k],
-            device_id={"pp": place.stage}, device_id_type=MESH) for k in range(2)]
+            src_ref=src, dst_ref=far_gain.at[k], send_sem=gain_send.at[k], recv_sem=gain_recv.at[k],
+            device_id={"pp": place.stage}, device_id_type=MESH) for k, src in enumerate([attn_gain, mlp_gain])]
     for copy in gain_copies:
         copy.start()
+    each(qkv_u + o_u, "start")
     each(gate_u + up_u + dn_u + next_u, "start")
     each(crossing, "start")
     for copy in loads[3:5]:
@@ -405,8 +404,7 @@
     cos_t[...] = jnp.cos(angle)
     sin_t[...] = jnp.sin(angle)
     flow.through(qkv_u[1], "send")
-    loads[0].wait()
-    for copy in gain_copies:
+    for copy in loads[:3] + gain_copies:
         copy.wait()
     first = place.pp == 0
     table = []
@@ -418,13 +416,14 @@
         gains[pl.ds(k, 1), :] = row
     first_norm[...] = norm_rows(hidden_buf[...].astype(F32), table[0])
     flow.through(qkv_u[-1], "relay")
+    flow.through(gate_u[0], "send")
     each(qkv_u, "arrive")
     project(qkv0[...], first_norm[...], cos_t[...], sin_t[...], head_dim, q_scr, k_scr, v_scr)
     for copy in loads[3:5]:
         copy.wait()
 
     lane = lax.broadcasted_iota(jnp.int32, k_first.shape[1:], 1)
-    marks = [(o_u[-1], "relay"), (gate_u[0], "relay"), (gate_u[1], "relay"), (gate_u[3], "send")]
+    marks = [(gate_u[1], "send"), (gate_u[2], "send"), (gate_u[3], "send"), (up_u[0], "send")]
     for tile, mark in enumerate(marks):
         seq0 = tile * SEQ_TILE
         k_cols, v_cols = k_scr[...].astype(BF16), v_scr[...].astype(BF16)
@@ -439,29 +438,31 @@
     each(o_u, "arrive")
     part[0] = dot_nn(attn[...], o_buf[...])
     sum_o.scatter_start()
-    flow.through(up_u[1], "relay")
+    flow.through(dn_u[0], "send")
     own_rows = hidden_buf[pl.ds(pl.multiple_of(place.tg * count, count), count), :]
     h_mid = (own_rows.astype(F32) + sum_o.total()).astype(BF16).astype(F32)
     sum_o.spread_start(norm_rows(h_mid, gains[2:3, :]))
-    flow.through(up_u[-1], "relay")
+    flow.through(dn_u[-1], "send")
+    each(next_u, "send")
     each(gate_u, "arrive")
     sum_o.spread_finish()
     act_in = mid[...]
     gate = jax.nn.silu(dot_nt(act_in, gate_buf[...]))
+    flow.through(dn_u[-1], "relay")
     each(up_u, "arrive")
     act = (gate * dot_nt(act_in, up_buf[...])).astype(BF16)
-    flow.through(dn_u[-1], "send")
-    each(next_u, "send")
-    flow.through(dn_u[-1], "relay")
     each(dn_u, "arrive")
     part[1] = dot_nn(act, dn_buf[...])
     sum_d.scatter_start()
-    each(next_u[:4], "relay")
+    each(next_u[:late], "relay")
+    each(next_u[:late // 2], "receive")
     h_new = (h_mid + sum_d.total()).astype(BF16)
     h_out[...] = h_new
     sum_d.spread_start(norm_rows(h_new.astype(F32), gains[1:2, :]))
-    each(next_u[4:], "relay")
+    each(next_u[late:], "relay")
+    each(next_u[late // 2:late], "receive")
     each(now_u, "finish")
+    each(next_u[late:], "receive")
     each(crossing, "finish")
     sum_d.spread_finish()
     each(next_u, "arrive")
@@ -470,12 +471,13 @@
         copy.wait()
 
 
-def attend_kernel(head_dim, lens, normed, w_qkv, cos_t, sin_t, k_in, v_in, w_first, gate, up, k_first, v_first,
+def attend_kernel(head_dim, lens, normed, w_qkv, cos_t, sin_t, k_in, v_in, w_first, gate, up, gate1, k_first, v_first,
                   k_out, v_out, gen_qkv, gen_gu, attn_out, k_new, v_new, q_scr, k_scr, v_scr, kv_sem, gen_sem):
     ffn = gate.shape[0]
     gens = [pltpu.make_async_copy(src, dst, gen_sem.at[k]) for k, (src, dst) in enumerate([
         (k_first, k_out.at[0]), (v_first, v_out.at[0]), (w_first, gen_qkv.at[0]), (w_qkv, gen_qkv.at[1]),
-        (gate, gen_gu.at[0, pl.ds(0, ffn)]), (up, gen_gu.at[0, pl.ds(ffn, ffn)])])]
+        (gate, gen_gu.at[0, pl.ds(0, ffn)]), (up, gen_gu.at[0, pl.ds(ffn, ffn)]),
+        (gate1, gen_gu.at[1, pl.ds(0, ffn)])])]
     for copy in gens:
         copy.start()
     batch, width = q_scr.shape
@@ -513,14 +515,13 @@
         copy.wait()
 
 
-def last_layer_kernel(tg_size, sizes, attn, h_in, gains, o1, gate_held, up_held, dn_held, w_gu, w_dn,
-                      hidden_out, gate_buf, up_buf, dn_buf, part, slots, mid, sum_send, sum_recv, *sems):
+def last_layer_kernel(tg_size, sizes, attn, h_in, gains, o1, gate1, up_held, dn_held, w_gu, w_dn,
+                      hidden_out, up_buf, dn_buf, part, slots, mid, sum_send, sum_recv, *sems):
     place = Place(tg_size)
     make = Maker(place, sems, sizes)
-    gate_u = make.gather("gate", 1, w_gu, gate_buf, HALVES, gate_held)
     up_u = make.gather("up", 1, w_gu, up_buf, HALVES, up_held)
     dn_u = make.gather("dn", 1, w_dn, dn_buf, HALVES, dn_held)
-    every = gate_u + up_u + dn_u
+    every = up_u + dn_u
     sum_o = SumOverTg(place, part.at[0], slots.at[0], mid, (sum_send.at[0], sum_recv.at[0]))
     sum_d = SumOverTg(place, part.at[1], slots.at[1], hidden_out, (sum_send.at[1], sum_recv.at[1]))
 
@@ -529,17 +530,14 @@
     part[0] = dot_nn(attn[...], o1[...])
     sum_o.scatter_start()
     each(every, "send")
-    each(gate_u, "relay")
+    each(up_u, "relay")
     h_mid = (h_in[...].astype(F32) + sum_o.total()).astype(BF16).astype(F32)
     sum_o.spread_start(norm_rows(h_mid, gains[3:4, :]))
-    each(gate_u, "receive")
-    each(up_u, "relay")
-    each(gate_u, "arrive")
+    each(up_u, "receive")
+    each(dn_u, "relay")
     sum_o.spread_finish()
     act_in = mid[...]
-    gate = jax.nn.silu(dot_nt(act_in, gate_buf[...]))
-    each(dn_u, "relay")
-    each(up_u, "receive")
+    gate = jax.nn.silu(dot_nt(act_in, gate1[...]))
     each(up_u, "arrive")
     act = (gate * dot_nt(act_in, up_buf[...])).astype(BF16)
     each(dn_u, "receive")
@@ -552,10 +550,10 @@
     sum_d.spread_finish()
 
 
-def store_kernel(layer, gate, up, prior, gen_gu, sem):
-    ffn = gate.shape[0]
-    copies = [pltpu.make_async_copy(src, gen_gu.at[layer, pl.ds(k * ffn, ffn)], sem.at[k])
-              for k, src in enumerate([gate, up])]
+def store_kernel(up, hidden, prior, gen_gu, hidden_out, sem):
+    ffn = up.shape[0]
+    copies = [pltpu.make_async_copy(src, dst, sem.at[k]) for k, (src, dst) in enumerate([
+        (up, gen_gu.at[1, pl.ds(ffn, ffn)]), (hidden, hidden_out)])]
     for copy in copies:
         copy.start()
     for copy in copies:
@@ -607,17 +605,17 @@
         off_chip = lambda like: pltpu.HBM(like.shape, like.dtype)
         hbm = lambda *arrays: [pltpu.with_memory_space_constraint(arr, pltpu.HBM) for arr in arrays]
         vmem = lambda *arrays: [pltpu.with_memory_space_constraint(arr, pltpu.VMEM) for arr in arrays]
-        shared = [act, sds((quarter, dim), BF16), sds((4, dim), F32), rope, rope, merged_ffn, merged_ffn,
+        shared = [act, sds((quarter, dim), BF16), sds((4, dim), F32), rope, rope, merged_ffn, merged_ffn, merged_ffn,
                   merged_qkv, merged_qkv, merged_o, layer_kv, layer_kv, layer_kv, layer_kv]
-        (normed, h_own, gains, cos_t, sin_t, gate0, up0, qkv0, qkv1, o1, k_first, v_first, k_next, v_next,
-         gate_held, up_held, dn_held) = pl.pallas_call(
+        (normed, h_own, gains, cos_t, sin_t, gate0, up0, gate1, qkv0, qkv1, o1, k_first, v_first, k_next, v_next,
+         up_held, dn_held) = pl.pallas_call(
             functools.partial(opening_kernel, tg_size, sizes),
-            in_specs=[SMEM, VMEM] + [HBM] * 9, out_specs=[VMEM] * 14 + [HBM] * 3,
-            out_shape=[on_chip(x) for x in shared] + [off_chip(held)] * 3,
+            in_specs=[SMEM, VMEM] + [HBM] * 9, out_specs=[VMEM] * 15 + [HBM] * 2,
+            out_shape=[on_chip(x) for x in shared] + [off_chip(held)] * 2,
             scratch_shapes=[pltpu.VMEM((width, dim), BF16), pltpu.VMEM((ffn, dim), BF16)] + sum_scratch + [
                 pltpu.VMEM((batch, dim), BF16), pltpu.VMEM((batch, dim), BF16), pltpu.VMEM((batch, width), BF16)]
             + projected + [pltpu.VMEM((2, 1, dim), BF16), pltpu.VMEM((2, 1, dim), BF16),
-                           dma((7,)), dma((2,)), dma((2,))] + sum_sems + gather_sems(31),
+                           dma((7,)), dma((2,)), dma((2,))] + sum_sems + gather_sems(34),
             compiler_params=remote_params(1, OPENING_VMEM), name="opening",
         )(seq_lens, seq_lens.reshape(1, batch), *hbm(hidden_in, attn_gain, mlp_gain, w_qkv, w_o_t, w_gate_up, w_down_t,
                                                      k_flat, v_flat))
@@ -625,27 +623,27 @@
         cache_shape = off_chip(k_flat)
         k_out, v_out, gen_qkv, gen_gate_up, attn = pl.pallas_call(
             functools.partial(attend_kernel, head_dim),
-            in_specs=[SMEM] + [VMEM] * 11, out_specs=[HBM] * 4 + [VMEM],
+            in_specs=[SMEM] + [VMEM] * 12, out_specs=[HBM] * 4 + [VMEM],
             out_shape=[cache_shape, cache_shape, pltpu.HBM((layers, 3 * width, dim), BF16),
                        pltpu.HBM((layers, 2 * ffn, dim), BF16), pltpu.VMEM((batch, width), BF16)],
             scratch_shapes=[pltpu.VMEM(layer_kv.shape, BF16)] * 2 + projected + [
-                dma((2, batch // SEQ_TILE)), dma((6,))],
+                dma((2, batch // SEQ_TILE)), dma((7,))],
             compiler_params=pltpu.CompilerParams(vmem_limit_bytes=ATTEND_VMEM), name="attend",
-        )(seq_lens, *vmem(normed, qkv1, cos_t, sin_t, k_next, v_next, qkv0, gate0, up0, k_first, v_first))
-
-        hidden, gate1, up1 = pl.pallas_call(
+        )(seq_lens, *vmem(normed, qkv1, cos_t, sin_t, k_next, v_next, qkv0, gate0, up0, gate1, k_first, v_first))
+
+        hidden, up1 = pl.pallas_call(
             functools.partial(last_layer_kernel, tg_size, sizes),
-            in_specs=[VMEM] * 4 + [HBM] * 5, out_specs=[VMEM] * 3,
-            out_shape=[on_chip(act), on_chip(merged_ffn), on_chip(merged_ffn)],
-            scratch_shapes=[pltpu.VMEM((ffn, dim), BF16)] + sum_scratch + sum_sems + gather_sems(12),
+            in_specs=[VMEM] * 5 + [HBM] * 4, out_specs=[VMEM] * 2,
+            out_shape=[on_chip(act), on_chip(merged_ffn)],
+            scratch_shapes=[pltpu.VMEM((ffn, dim), BF16)] + sum_scratch + sum_sems + gather_sems(8),
             compiler_params=remote_params(2, LAST_VMEM), name="layer_1",
-        )(*vmem(attn, h_own, gains, o1), *hbm(gate_held, up_held, dn_held, w_gate_up, w_down_t))
-
-        gen_gate_up = pl.pallas_call(
-            functools.partial(store_kernel, 1),
-            in_specs=[VMEM, VMEM, HBM], out_specs=HBM, out_shape=pltpu.HBM(gen_gate_up.shape, BF16),
+        )(*vmem(attn, h_own, gains, o1, gate1), *hbm(up_held, dn_held, w_gate_up, w_down_t))
+
+        gen_gate_up, hidden = pl.pallas_call(
+            store_kernel, in_specs=[VMEM, VMEM, HBM], out_specs=[HBM, HBM],
+            out_shape=[pltpu.HBM(gen_gate_up.shape, BF16), off_chip(act)],
             scratch_shapes=[dma((2,))], input_output_aliases={2: 0}, name="store",
-        )(*vmem(gate1, up1), gen_gate_up)
+        )(*vmem(up1, hidden), gen_gate_up)
 
         unflat = lambda cache: jnp.transpose(
             cache.reshape(layers, batch, kv_loc, head_dim, cache_len), (0, 1, 4, 2, 3))

time: 119 us -> 108 us (0.908)
  Pallas kernels: 118 us -> 106 us
    pallas_call x1, Pallas kernels: 71.6 us -> 65.7 us  [body(): pl.pallas_call(functools.partial(opening_kernel, tg_size, sizes), in_spec...]
    pallas_call x1, Pallas kernels: 36.3 us -> 30.7 us  [body(): pl.pallas_call(functools.partial(last_layer_kernel, tg_size, sizes), in_s...]
where the time goes in v4:
time: 108 us; the launch traced here: 107 us
  Pallas kernels  106 us (98%)
    pallas_call x1, Pallas kernels, body(): pl.pallas_call(functools.partial(opening_kernel, tg_size, sizes), in_spec...  65.7 us
    pallas_call x1, Pallas kernels, body(): pl.pallas_call(functools.partial(last_layer_kernel, tg_size, sizes), in_s...  30.7 us
    pallas_call x1, Pallas kernels, body(): pl.pallas_call(functools.partial(attend_kernel, head_dim), in_specs=[SMEM...  8.88 us

profile of v4, /device:TPU:0, one launch (start us, length us, event | category | flops | bytes accessed | tf_op | source)
XLA Modules:
  0.0 107.1 jit_solution(17651433985789787190)
XLA Ops:
  0.6 65.7 %opening.1 = (bf16[64,1024]{1,0:T(8,128)(2,1)S(1)}, bf16[16,1024]{1,0:T(8,128)(2,1)S(1)}, f32[4,1024]{1,0:T(4,128)S(1)}, f32[32,64]{1,0:T(8,128)S(1)}, f32[32,64...) custom-call(s32[64]{0:T(128)} %lens.3, ...), custom_call_target="tpu_custom_call" | custom-call | tf_op jit(solution)/shard_map/opening/pallas_call | solution.py:611
  66.4 8.9 %attend.1 = (bf16[2,64,256,128]{3,2,1,0:T(8,128)(2,1)}, bf16[2,64,256,128]{3,2,1,0:T(8,128)(2,1)}, bf16[2,768,1024]{2,1,0:T(8,128)(2,1)}, bf16[2,1408,1024]{2,1,0:T(8,128)(2,1)}, bf16[64,256]{1,0:T(8,128)(2,1)S(1)}) custom-call(s32[64]{0:T(128)} %lens.3, bf16[64,1024]{1,0:T(8,128)(2,1)S(1)} %get-tuple-element.31.normed, ...), custom_call_target="tpu_custom_call" | custom-call | tf_op jit(solution)/shard_map/attend/pallas_call | solution.py:624
  75.2 30.7 %layer_1.1 = (bf16[64,1024]{1,0:T(8,128)(2,1)S(1)}, bf16[704,1024]{1,0:T(8,128)(2,1)S(1)}) custom-call(bf16[64,256]{1,0:T(8,128)(2,1)S(1)} %get-tuple-element.43.attn, bf16[16,1024]{1,0:T(8,128)(2,1)S(1)} %get-tuple-element.44.h_in, f32[4,1024]{1,0:T(4,128)S(1)} %get-tuple-element.45.gains, bf16[256,1024]{1,0:T(8,128)(2,1)S(1)} %get-tuple-element.46.o1, ...), custom_call_target="tpu_custom_call" | custom-call | tf_op jit(solution)/shard_map/layer_1/pallas_call | solution.py:634
  106.0 1.2 %store.1 = (bf16[2,1408,1024]{2,1,0:T(8,128)(2,1)}, bf16[64,1024]{1,0:T(8,128)(2,1)}) custom-call(bf16[704,1024]{1,0:T(8,128)(2,1)S(1)} %get-tuple-element.49.up, bf16[64,1024]{1,0:T(8,128)(2,1)S(1)} %get-tuple-element.50.hidden, bf16[2,1408,1024]{2,1,0:T(8,128)(2,1)} %get-tuple-element.51.prior), custom_call_target="tpu_custom_call", output_to_operand_aliasing={{0}: (2, {})} | custom-call | tf_op jit(solution)/shard_map/store/pallas_call | solution.py:642
